TPU v7x, 256 devices: a whole 4x4x8 slice. The times are simulated.
256 devices in a mesh: dp: 64 (over z, y, core), mp: 4 (over x).
Axes of the slice: x: 4, y: 4, z: 8, core: 2. Of those that a mesh axis runs over, the one named last changes fastest.
Arguments:
- tokens: bfloat16 [393216, 512], P('dp'), may hold values from -6 to 6
- w_uvqk: bfloat16 [512, 2048], P(None, 'mp')
- w_out: bfloat16 [512, 512], replicated, may hold values from -0.25 to 0.25
- hist_len: int32 [64, 24], P('dp'), may hold values from 64 to 256, as said below
- owner: int32 [64, 24], P('dp'), may hold values from 0 to 63, as said below
- recv_offset: int32 [64, 24], P('dp'), may hold values from 0 to 47, as said below
- block_start: int32 [64, 24], P('dp'), may hold values from 0 to 47, as said below
Outputs:
- packed_out: bfloat16 [393216, 512], P('dp', 'mp')
- user_state: bfloat16 [1536, 512], P('dp', 'mp')
Inputs may be any that keep to these rules, and one draw needn't show every extreme that they name: User (d, u) has ceil(hist_len / 128) blocks, at most 2. owner[d, u] = (p(d) + r(u mod 64)) mod 64 for two permutations p, r of the indices of dp drawn from the seed: every owner receives exactly 24 users, and one device sends at most 1 users to one owner. On some owner every received user has 2 blocks. `recv_offset`: the users of one owner occupy disjoint runs of its 48 blocks, in the order of u; on some owner they fill all 48 blocks. `block_start`: the users of one device occupy disjoint runs of its 48 blocks, in the order of u.
All inputs are finite; a program needn't handle non-finite values.
Results may differ from a plain program's by a relative error of at most 0.0059.
Values may be sent and summed in bfloat16 or wider, within the bound.
A program may use at most 128 MiB of HBM per device.

v0:
```python
import jax
import jax.numpy as jnp
from jax import lax
from jax.sharding import PartitionSpec as P

D = 512
HEADS = 4
BLOCK = 128
MAXB = 2
BLK_DEV = 48


EPS = 1e-05


def sent_to_all(shard, axis):
    count = lax.axis_size(axis)
    return lax.all_to_all(
        jnp.broadcast_to(shard[None], (count, *shard.shape)), axis, 0, 0, tiled=True
    )


def over_copies(shard, axis):
    everything = sent_to_all(shard, axis)
    return jnp.sum(everything, axis=0)


def together(arrays, axis):
    ends = [0]
    for a in arrays:
        ends.append(ends[-1] + a.size)
    subtotal = over_copies(jnp.concatenate([a.ravel() for a in arrays]), axis)
    return tuple((subtotal[b:e].reshape(a.shape) for a, b, e in zip(arrays, ends, ends[1:])))


def in_one_piece(arrays, axis, dim, along):
    widths = [a.shape[along] for a in arrays]
    both = jnp.concatenate(arrays, axis=along)
    result = lax.all_gather(both, axis, axis=dim, tiled=True)
    return tuple(jnp.split(result, [sum(widths[:k]) for k in range(1, len(widths))], axis=along))


def norm_rows(values):
    average = jnp.mean(values, axis=-1, keepdims=True)
    variance = jnp.mean(values * values, axis=-1, keepdims=True) - average * average
    return (values - average) * lax.rsqrt(variance + EPS)


def attend(query, keys, values, query_user, key_user):
    row_count, head_size = query.shape
    tile_rows = 4 * BLOCK
    back_rows = (MAXB - 1) * BLOCK
    scaling = (D // HEADS) ** (-0.5)
    keys_ext = jnp.concatenate([jnp.zeros((back_rows, head_size), keys.dtype), keys], 0)
    values_ext = jnp.concatenate([jnp.zeros((back_rows, head_size), values.dtype), values], 0)
    users_ext = jnp.concatenate([jnp.full((back_rows,), -2, jnp.int32), key_user], 0)
    query_pos = jnp.arange(tile_rows, dtype=jnp.int32)[:, None] + back_rows
    key_pos = jnp.arange(tile_rows + back_rows, dtype=jnp.int32)[None, :]

    def one_tile(start):
        query_tile = lax.dynamic_slice_in_dim(query, start, tile_rows, 0)
        key_tile = lax.dynamic_slice_in_dim(keys_ext, start, tile_rows + back_rows, 0)
        value_tile = lax.dynamic_slice_in_dim(values_ext, start, tile_rows + back_rows, 0)
        query_owner = lax.dynamic_slice_in_dim(query_user, start, tile_rows, 0)
        key_owner = lax.dynamic_slice_in_dim(users_ext, start, tile_rows + back_rows, 0)
        raw_scores = (
            lax.dot_general(
                query_tile, key_tile, (((1,), (1,)), ((), ())), preferred_element_type=jnp.float32
            )
            * scaling
        )
        allowed = (query_owner[:, None] == key_owner[None, :]) & (key_pos <= query_pos)
        weights = jnp.where(allowed, jax.nn.silu(raw_scores) / (MAXB * BLOCK), 0.0).astype(
            jnp.bfloat16
        )
        return jnp.dot(weights, value_tile, preferred_element_type=jnp.float32)

    tile_starts = jnp.arange(row_count // tile_rows, dtype=jnp.int32) * tile_rows
    return lax.map(one_tile, tile_starts).reshape(row_count, head_size)


def layer_rows(rows_in, query_user, key_user, w_uvqk, w_out):
    row_count = rows_in.shape[0]
    head_size = D // HEADS
    mp_size = lax.axis_size("mp")
    portion = lax.axis_index("mp")
    quarter = D // mp_size
    local_heads = w_uvqk.shape[1] // (4 * head_size)
    widened = rows_in.astype(jnp.float32)
    normed = norm_rows(widened).astype(jnp.bfloat16)
    projected = jax.nn.silu(jnp.dot(normed, w_uvqk, preferred_element_type=jnp.float32)).astype(
        jnp.bfloat16
    )
    pieces = projected.reshape(row_count, local_heads, 4, head_size)
    outputs = attend(pieces[:, 0, 2], pieces[:, 0, 3], pieces[:, 0, 1], query_user, key_user)
    totals = together((jnp.sum(outputs, 1), jnp.sum(outputs * outputs, 1)), "mp")
    average = totals[0] / D
    variance = totals[1] / D - average * average
    gates = pieces[:, :, 0].reshape(row_count, local_heads * head_size).astype(jnp.float32)
    gated_rows = ((outputs - average[:, None]) * lax.rsqrt(variance + EPS)[:, None] * gates).astype(
        jnp.bfloat16
    )
    every_head = lax.all_gather(gated_rows, "mp", axis=1, tiled=True)
    out_columns = lax.dynamic_slice_in_dim(w_out, portion * quarter, quarter, 1)
    mixed_rows = jnp.dot(every_head, out_columns, preferred_element_type=jnp.float32)
    residual = lax.dynamic_slice_in_dim(widened, portion * quarter, quarter, 1)
    return (mixed_rows + residual).astype(jnp.bfloat16)


def row_labels(block_user, block_fill):
    in_block = jnp.arange(BLOCK, dtype=jnp.int32)[None, :]
    row_live = (in_block < block_fill[:, None]).reshape(-1)
    row_user = jnp.broadcast_to(block_user[:, None], (block_user.shape[0], BLOCK)).reshape(-1)
    return (row_live, jnp.where(row_live, row_user, -3), jnp.where(row_live, row_user, -2))


def per_device(tokens, w_uvqk, w_out, hist_len, owner, recv_offset, block_start):
    dp_size = lax.axis_size("dp")
    mp_size = lax.axis_size("mp")
    myself = lax.axis_index("dp")
    user_count = hist_len.shape[1]
    per_pair = -(-user_count // dp_size)
    pair_cap = per_pair * MAXB
    quarter = D // mp_size
    lengths = hist_len[0]
    owners = owner[0]
    starts = block_start[0]
    counts = (lengths + BLOCK - 1) // BLOCK
    user_ids = jnp.arange(user_count, dtype=jnp.int32)
    earlier = user_ids[None, :] < user_ids[:, None]
    same_owner = (owners[:, None] == owners[None, :]) & earlier
    in_pair = jnp.sum(jnp.where(same_owner, counts[None, :], 0), axis=1)
    slot_ids = jnp.arange(pair_cap, dtype=jnp.int32)
    device_ids = jnp.arange(dp_size, dtype=jnp.int32)
    slot_step = slot_ids[None, :, None] - in_pair[None, None, :]
    sending = (
        (owners[None, None, :] == device_ids[:, None, None])
        & (slot_step >= 0)
        & (slot_step < counts[None, None, :])
    )
    send_block = jnp.sum(jnp.where(sending, starts[None, None, :] + slot_step, 0), axis=2)
    all_len, all_owner, all_offset = in_one_piece((hist_len, owner, recv_offset), "dp", 0, 1)
    all_counts = (all_len + BLOCK - 1) // BLOCK
    all_before = (all_owner[:, :, None] == all_owner[:, None, :]) & earlier[None]
    all_in_pair = jnp.sum(jnp.where(all_before, all_counts[:, None, :], 0), axis=2)
    owned = all_owner == myself
    flat_owned = owned.reshape(-1)
    flat_len = all_len.reshape(-1)
    flat_offset = all_offset.reshape(-1)
    flat_counts = all_counts.reshape(-1)
    flat_in_pair = all_in_pair.reshape(-1)
    candidate_ids = jnp.arange(dp_size * user_count, dtype=jnp.int32)
    source_ids = candidate_ids // user_count
    block_ids = jnp.arange(BLK_DEV, dtype=jnp.int32)
    land_step = block_ids[:, None] - flat_offset[None, :]
    landed = flat_owned[None, :] & (land_step >= 0) & (land_step < flat_counts[None, :])
    slot_index = jnp.sum(
        jnp.where(landed, source_ids[None, :] * pair_cap + flat_in_pair[None, :] + land_step, 0),
        axis=1,
    )
    owned_user = jnp.sum(jnp.where(landed, candidate_ids[None, :], 0), axis=1)
    owned_fill = jnp.sum(
        jnp.where(landed, jnp.clip(flat_len[None, :] - land_step * BLOCK, 0, BLOCK), 0), axis=1
    )
    owned_live, owned_query, owned_key = row_labels(owned_user, owned_fill)
    local_step = block_ids[:, None] - starts[None, :]
    within = (local_step >= 0) & (local_step < counts[None, :])
    local_user = jnp.sum(jnp.where(within, user_ids[None, :], 0), axis=1)
    local_fill = jnp.sum(
        jnp.where(within, jnp.clip(lengths[None, :] - local_step * BLOCK, 0, BLOCK), 0), axis=1
    )
    local_live, local_query, local_key = row_labels(local_user, local_fill)
    results = layer_rows(tokens, local_query, local_key, w_uvqk, w_out)
    state = jnp.take(results, starts * BLOCK + lengths - 1, axis=0)
    outgoing = jnp.take(results.reshape(BLK_DEV, BLOCK, quarter), send_block, axis=0)
    arrived = lax.all_to_all(outgoing, "dp", split_axis=0, concat_axis=0, tiled=True)
    gathered = jnp.take(
        arrived.reshape(dp_size * pair_cap, BLOCK, quarter), slot_index, axis=0
    ).reshape(BLK_DEV * BLOCK, quarter)
    packed = jnp.where(owned_live[:, None], gathered, jnp.zeros_like(gathered))
    return (packed, state)


def solution(mesh):
    in_specs = (
        P("dp", None),
        P(None, "mp"),
        P(),
        P("dp", None),
        P("dp", None),
        P("dp", None),
        P("dp", None),
    )
    out_specs = (P("dp", "mp"), P("dp", "mp"))
    return jax.shard_map(
        per_device, mesh=mesh, in_specs=in_specs, out_specs=out_specs, check_vma=False
    )
```

profile of v0, /device:TPU:1, one launch (start us, length us, event | category | flops | bytes accessed | tf_op | source)
XLA Modules:
  0.0 370.8 jit_solution(17628559279992237693)
XLA Ops:
  7.2 4.8 %convert_reduce_fusion = (f32[6144]{0:T(1024)S(1)}, f32[6144]{0:T(1024)S(1)}) fusion(bf16[6144,512]{1,0:T(8,128)(2,1)} %param.9), kind=kLoop, calls=%fused_computation.31 | loop fusion | flops 12570624 | bytes 6340608 | tf_op jit(solution)/shard_map/reduce_sum | solution.py:44
  12.0 8.0 %multiply_convert_fusion = bf16[6144,512]{0,1:T(8,128)(2,1)S(1)} fusion(bf16[512,512]{1,0:T(8,128)(2,1)S(1)} %copy-done, bf16[6144,512]{1,0:T(8,128)(2,1)S(1)} %copy-done.2, f32[6144]{0:T(1024)S(1)} %get-tuple-element.108, f32[6144]{0:T(1024)S(1)} %get-tuple-element.107), kind=kOutput, calls=%fused_computation.28 | convolution fusion | flops 3249537024 | bytes 13156352 | tf_op jit(solution)/shard_map/dot_general | solution.py:91
  20.0 2.3 fusion.59
  22.3 1.3 copy-done.3
  23.7 2.6 copy.50
  26.3 2.6 copy.51
  28.9 2.8 concatenate.17
  31.7 1.3 concatenate.18
  33.0 1.6 copy.49
  34.7 78.6 %while.11 = (s32[]{:T(128)}, f32[12,512,128]{2,1,0:T(8,128)}, s32[12]{0:T(128)S(1)}, s32[6144]{0:T(1024)S(1)}, s32[6272]{0:T(1024)S(1)}, /*index=5*/bf16[6144,12...) while((s32[]{:T(128)}, f32[12,512,128]{2,1,0:T(8,128)}, ...), condition=%wide.region_10.11_spmd.clone, body=%wide.region_9.10_spmd.clone.sunk | while | flops 171377152 | bytes 741060 | solution.py:79
  34.8 0.6 dynamic_slice.53
  38.7 2.6 fusion.70
  41.3 0.6 dynamic_slice.53
  45.3 2.6 fusion.70
  47.9 0.6 dynamic_slice.53
  51.8 2.6 fusion.70
  54.4 0.6 dynamic_slice.53
  58.4 2.6 fusion.70
  61.0 0.6 dynamic_slice.53
  64.9 2.6 fusion.70
  67.5 0.6 dynamic_slice.53
  71.5 2.6 fusion.70
  74.1 0.6 dynamic_slice.53
  78.0 2.6 fusion.70
  80.6 0.6 dynamic_slice.53
  84.5 2.6 fusion.70
  87.2 0.6 dynamic_slice.53
  91.1 2.6 fusion.70
  93.7 0.6 dynamic_slice.53
  97.7 2.6 fusion.70
  104.2 2.6 fusion.70
  110.8 2.6 fusion.70
  113.4 3.6 fusion.58
  117.0 0.8 broadcast_in_dim.174
  117.8 4.8 %all-to-all-start = ((f32[4,1,12288]{2,1,0:T(1,128)}), f32[4,1,12288]{2,1,0:T(1,128)S(1)}, u32[]{:S(2)}, u32[]{:S(2)}) async-start(f32[4,1,12288]{2,1,0:T(1,128)} %broadcast_in_dim.174), calls=%async_computation | async-start | bytes 393216 | tf_op jit(solution)/shard_map/all_to_all | solution.py:18
  122.6 3.5 copy.46
  126.2 1.6 all-to-all-done
  128.0 4.0 %fusion.30 = bf16[6144,128]{0,1:T(8,128)(2,1)} fusion(f32[6144,128]{0,1:T(8,128)} %copy.46, bf16[6144,1,4,128]{0,3,2,1:T(8,128)(2,1)} %bitcast.68, f32[6144]{0:T(1024)S(1)} %get-tuple-element.102, f32[6144]{0:T(1024)S(1)} %get-tuple-element.101), kind=kLoop, calls=%fused_computation.39 | loop fusion | flops 3932160 | bytes 6340608 | tf_op jit(solution)/shard_map/convert_element_type | solution.py:100
  132.0 9.2 %convert_element_type.24 = f32[6144,512]{1,0:T(8,128)} convert(bf16[6144,512]{1,0:T(8,128)(2,1)} %param.9) | non-fusion elementwise | flops 3145728 | bytes 18874368 | tf_op jit(solution)/shard_map/convert_element_type | solution.py:89
  142.0 60.7 %all-gather.3.cloned.1.call-done = bf16[6144,512]{0,1:T(8,128)(2,1)} async-done(((bf16[6144,128]{0,1:T(8,128)(2,1)}), bf16[6144,512]{0,1:T(8,128)(2,1)}) %all-gather.3.cloned.1.call-update) | async-done | bytes 6291472 | tf_op jit(solution)/shard_map/all_gather | solution.py:103
  202.7 5.6 %fusion.26 = bf16[6144,128]{1,0:T(8,128)(2,1)S(1)} fusion(bf16[6144,512]{0,1:T(8,128)(2,1)} %all-gather.3.cloned.1.call-done, f32[6144,512]{1,0:T(8,128)} %convert_element_type.24, s32[]{:T(128)S(6)} %select_n.164, bf16[512,512]{1,0:T(8,128)(2,1)} %param.11), kind=kOutput, calls=%fused_computation.33 | convolution fusion | flops 806879232 | bytes 11142144 | tf_op jit(solution)/shard_map/dot_general | solution.py:105
  208.4 3.1 gather_fusion
  211.4 4.6 %broadcast_select_fusion = bf16[64,2,128,128]{3,2,1,0:T(8,128)(2,1)} fusion(bf16[64,2,128,128]{3,2,1,0:T(8,128)(2,1)} %bitcast.65, pred[64,2]{1,0:T(8,128)(4,1)S(1)} %copy.41), kind=kLoop, calls=%fused_computation.37 | loop fusion | flops 2097152 | bytes 8388736 | tf_op jit(solution)/shard_map/jit(_take)/select_n | solution.py:175
  216.0 11.2 %all-to-all-start.1 = ((bf16[64,2,128,128]{3,2,1,0:T(8,128)(2,1)}), bf16[64,2,128,128]{3,2,1,0:T(8,128)(2,1)}, u32[]{:S(2)}, u32[]{:S(2)}) async-start(bf16[64,2,128,128]{3,2,1,0:T(8,128)(2,1)} %broadcast_select_fusion), calls=%async_computation.1 | async-start | bytes 8388608 | tf_op jit(solution)/shard_map/all_to_all | solution.py:176
  227.3 125.6 %all-gather = s32[64,1,72]{2,1,0:T(1,128)S(1)} all-gather(s32[1,1,72]{2,1,0:T(1,128)S(1)} %add_bitcast_fusion), channel_id=1, replica_groups=mesh['dp'=64,'mp'=4] {'dp'}, dimensions={0}, use_global_device_ids=true | all-gather | bytes 18720 | tf_op jit(solution)/shard_map/all_gather | solution.py:39
  355.0 0.7 broadcast_select_fusion.1
  355.6 3.1 gather_fusion.1
  358.7 5.2 %fusion.31 = bf16[6144,128]{1,0:T(8,128)(2,1)} fusion(bf16[48,128,128]{2,1,0:T(8,128)(2,1)S(1)} %gather_fusion.1, pred[6144]{0:T(1024)(128)(4,1)S(1)} %get-tuple-element.114, pred[6144]{0:T(1024)(128)(4,1)S(1)} %get-tuple-element.113), kind=kLoop, calls=%fused_computation.43 | loop fusion | flops 1572864 | bytes 3158016 | tf_op jit(solution)/shard_map/jit(_where)/select_n | solution.py:180
  (105 shorter events, 6.5 us)
Async XLA Ops:
  7.2 4.8 %copy-start = (bf16[512,512]{1,0:T(8,128)(2,1)S(1)}, bf16[512,512]{1,0:T(8,128)(2,1)}, u32[]{:S(2)}) copy-start(bf16[512,512]{1,0:T(8,128)(2,1)} %param.10) | copy-start | bytes 1572868
  7.2 4.8 %copy-start.2 = (bf16[6144,512]{1,0:T(8,128)(2,1)S(1)}, bf16[6144,512]{1,0:T(8,128)(2,1)}, u32[]{:S(2)}) copy-start(bf16[6144,512]{1,0:T(8,128)(2,1)} %param.9) | copy-start | bytes 18874372
  20.0 3.7 copy-start.3
  28.9 2.8 copy-start.4
  31.7 2.8 copy-start.6
  31.7 2.8 copy-start.7
  117.8 10.0 %all-to-all-start = ((f32[4,1,12288]{2,1,0:T(1,128)}), f32[4,1,12288]{2,1,0:T(1,128)S(1)}, u32[]{:S(2)}, u32[]{:S(2)}) async-start(f32[4,1,12288]{2,1,0:T(1,128)} %broadcast_in_dim.174), calls=%async_computation | async-start | bytes 393216 | tf_op jit(solution)/shard_map/all_to_all | solution.py:18
  122.6 80.1 %all-gather.3.cloned.1.call-start = ((), (), s32[]{:S(2)}) async-start(), calls=%async_computation.2 | async-start | bytes 7864320 | tf_op jit(solution)/shard_map/all_gather | solution.py:103
  132.0 9.2 %copy-start.5 = (s32[1,24]{1,0:T(1,128)S(1)}, s32[1,24]{1,0:T(1,128)}, u32[]{:S(2)}) copy-start(s32[1,24]{1,0:T(1,128)} %param.13) | copy-start | bytes 292
  216.0 11.2 %copy-start.8 = (s32[1,24]{1,0:T(1,128)S(1)}, s32[1,24]{1,0:T(1,128)}, u32[]{:S(2)}) copy-start(s32[1,24]{1,0:T(1,128)} %param.14) | copy-start | bytes 292
  216.0 139.6 %all-to-all-start.1 = ((bf16[64,2,128,128]{3,2,1,0:T(8,128)(2,1)}), bf16[64,2,128,128]{3,2,1,0:T(8,128)(2,1)}, u32[]{:S(2)}, u32[]{:S(2)}) async-start(bf16[64,2,128,128]{3,2,1,0:T(8,128)(2,1)} %broadcast_select_fusion), calls=%async_computation.1 | async-start | bytes 8388608 | tf_op jit(solution)/shard_map/all_to_all | solution.py:176
  355.6 8.3 %copy-start.1 = (bf16[512,512]{1,0:T(8,128)(2,1)S(1)}, bf16[512,512]{1,0:T(8,128)(2,1)}, u32[]{:S(2)}) copy-start(bf16[512,512]{1,0:T(8,128)(2,1)} %param.10) | copy-start | bytes 1572868
Sparse Core Ops, SparseCore 0:
  132.1 70.5 all-gather.2
where the time goes:
time: 372 us; the launch traced here: 371 us
  blocking collectives  126 us (34%)
  waiting for transfers between devices  62.4 us (17%)
  matrix products  45 us (12%)
  loops' own time  37.9 us (10%)
  local copies, waits for them, and re-layouts  35.9 us (10%)
  other arithmetic  33.7 us (9%)
  starting transfers between devices  16 us (4%)
  between operations  14.3 us (4%)
    all_gather x1, blocking collectives, in_one_piece(): result = lax.all_gather(both, axis, axis=dim, tiled=True)  126 us
    all_gather x1, waiting for transfers between devices, layer_rows(): every_head = lax.all_gather(gated_rows, 'mp', axis=1, tiled=True)  60.7 us
    another operation x1, loops' own time, attend(): return lax.map(one_tile, tile_starts).reshape(row_count, head_size)  37.9 us
    dot_general x12, matrix products, one_tile(): return jnp.dot(weights, value_tile, preferred_element_type=jnp.float32)  31.4 us
    all_to_all x1, starting transfers between devices, per_device(): lax.all_to_all(outgoing, 'dp', split_axis=0, concat_axis=0, tiled=True)  11.2 us
    convert_element_type x1, other arithmetic, layer_rows(): widened = rows_in.astype(jnp.float32)  9.17 us
    unnamed x21, local copies, waits for them, and re-layouts  8.13 us
    dot_general x1, matrix products, layer_rows(): jnp.dot(normed, w_uvqk, preferred_element_type=jnp.float32)  7.98 us
  transfers between devices with their start and end apart: 3, of which 2 were waited for; matrix products, arithmetic and copies ran while one was open for 4% of the time, Pallas kernels for 0%

commit v1 on v0

v1 whole, which is shorter than its diff:
```python
import functools

import jax
import jax.numpy as jnp
from jax import lax
from jax.experimental import pallas as pl
from jax.experimental.pallas import tpu as pltpu
from jax.sharding import PartitionSpec as P

D = 512
HEADS = 4
HEAD = 128
BLOCK = 128
WINDOW = 256
USERS = 24
BLK_DEV = 48
N_DP = 64
N_MP = 4
OWN = USERS // N_MP
CHUNKS = 2
UC = OWN // CHUNKS
TILE = 16
GROUPS = WINDOW // TILE
EPS = 1e-05
MESH = pl.DeviceIdType.MESH
BF16 = jnp.bfloat16
F32 = jnp.float32


def shift_of(i):
    return 2 * (i % 2) + (i // 2) % 2


def gated_silu(v):
    half = v * 0.5
    return half + half * jnp.tanh(half)


def main_kernel(
    tokens, w_in, w_out, len_v, own_v, off_v, len_s, own_s, start_s,
    landed, meta, states,
    tok, wbuf, wo, normed, att, gates, tab, pin_v, pin_s, st_send, st_recv, *rest,
):
    outgoing = rest[:CHUNKS]
    middle = rest[CHUNKS : 2 * CHUNKS]
    packed = rest[2 * CHUNKS : 3 * CHUNKS]
    (loc_sem, w_send, w_recv, f_send, f_recv, t_send, t_recv, s_send, s_recv,
     p1_send, p1_recv, p1_loc, p2_send, p2_recv, p2_loc, pin_sem) = rest[3 * CHUNKS :]
    me = lax.axis_index("dp")
    mp = lax.axis_index("mp")
    core = me % 2
    partner = me + 1 - 2 * core
    right = (mp + 1) % N_MP
    left = (mp + 3) % N_MP
    across = (mp + 2) % N_MP

    load_tok = pltpu.make_async_copy(tokens, tok, loc_sem.at[0])
    load_w = pltpu.make_async_copy(w_in, wbuf.at[mp], loc_sem.at[1])
    load_wo = pltpu.make_async_copy(w_out, wo, loc_sem.at[2])
    load_w.start()
    load_tok.start()
    load_wo.start()

    barrier = pltpu.get_barrier_semaphore()

    @pl.loop(1, N_DP)
    def _(t):
        pl.semaphore_signal(barrier, inc=1, device_id=((me + t) % N_DP, mp), device_id_type=MESH)

    for other in (right, left, across):
        pl.semaphore_signal(barrier, inc=1, device_id=(me, other), device_id_type=MESH)

    tab[me] = jnp.zeros((4, 128), jnp.int32)
    tab[me, 0:1, 0:USERS] = len_v[...]
    tab[me, 1:2, 0:USERS] = own_v[...]
    tab[me, 2:3, 0:USERS] = off_v[...]
    st_send[...] = jnp.zeros_like(st_send)

    load_tok.wait()

    def user_rows(k):
        start = start_s[0, mp * OWN + k]
        follow = jnp.minimum(start + 1, BLK_DEV - 1)
        return jnp.concatenate([tok[start], tok[follow]], axis=0).astype(F32)

    @pl.loop(0, OWN)
    def _(k):
        x = user_rows(k)
        mean = jnp.mean(x, axis=-1, keepdims=True)
        var = jnp.mean(x * x, axis=-1, keepdims=True) - mean * mean
        normed[k] = ((x - mean) * lax.rsqrt(var + EPS)).astype(BF16)

    load_w.wait()
    load_wo.wait()
    pl.semaphore_wait(barrier, N_DP - 1 + N_MP - 1)

    half = pl.ds(pl.multiple_of(core * 256, 256), 256)
    other_half = pl.ds(pl.multiple_of((1 - core) * 256, 256), 256)

    def send_w(shard, target, k):
        return pltpu.make_async_remote_copy(
            src_ref=wbuf.at[shard, half], dst_ref=wbuf.at[shard, half],
            send_sem=w_send.at[k], recv_sem=w_recv.at[k],
            device_id=(me, target), device_id_type=MESH,
        )

    def forward_w(shard, k):
        return pltpu.make_async_remote_copy(
            src_ref=wbuf.at[shard, half], dst_ref=wbuf.at[shard, half],
            send_sem=f_send.at[k], recv_sem=f_recv.at[k],
            device_id=(partner, mp), device_id_type=MESH,
        )

    to_right = send_w(mp, right, 0)
    to_left = send_w(mp, left, 1)
    to_right.start()
    to_left.start()

    @pl.loop(1, N_DP)
    def _(t):
        pltpu.make_async_remote_copy(
            src_ref=tab.at[me], dst_ref=tab.at[me], send_sem=t_send, recv_sem=t_recv,
            device_id=((me + t) % N_DP, mp), device_id_type=MESH,
        ).start()

    row_id = lax.broadcasted_iota(jnp.int32, (BLOCK, BLOCK), 0)
    col_id = lax.broadcasted_iota(jnp.int32, (BLOCK, BLOCK), 1)
    causal = col_id <= row_id
    scaling = float(HEAD) ** -0.5
    nt = (((1,), (1,)), ((), ()))

    def head_of_user(shard, k):
        projected = gated_silu(
            jnp.dot(normed[k], wbuf[shard], preferred_element_type=F32)
        ).astype(BF16)
        gates[k, shard] = projected[:, 0:HEAD]
        v = projected[:, HEAD : 2 * HEAD]
        q = projected[:, 2 * HEAD : 3 * HEAD]
        key = projected[:, 3 * HEAD :]
        diag = jnp.concatenate(
            [
                lax.dot_general(q[:BLOCK], key[:BLOCK], nt, preferred_element_type=F32),
                lax.dot_general(q[BLOCK:], key[BLOCK:], nt, preferred_element_type=F32),
            ],
            axis=0,
        )
        back = lax.dot_general(q[BLOCK:], key[:BLOCK], nt, preferred_element_type=F32)
        both = jnp.concatenate([causal, causal], axis=0)
        w_diag = jnp.where(both, gated_silu(diag * scaling), 0.0).astype(BF16)
        w_back = gated_silu(back * scaling).astype(BF16)
        att[k, shard, 0:BLOCK] = jnp.dot(w_diag[:BLOCK], v[:BLOCK], preferred_element_type=F32)
        att[k, shard, BLOCK:] = jnp.dot(
            jnp.concatenate([w_back, w_diag[BLOCK:]], axis=1), v, preferred_element_type=F32
        )

    def heads(shard):
        @pl.loop(0, OWN)
        def _(k):
            head_of_user(shard, k)

    heads(mp)

    to_right.wait_recv()
    from_left = forward_w(left, 0)
    from_left.start()
    to_left.wait_recv()
    from_right = forward_w(right, 1)
    from_right.start()
    onward_shard = jnp.where(core == 0, left, right)
    onward_target = jnp.where(core == 0, right, left)
    onward = send_w(onward_shard, onward_target, 2)
    onward.start()
    from_left.wait_recv()
    heads(left)
    from_right.wait_recv()
    onward.wait_recv()
    from_across = forward_w(across, 2)
    from_across.start()
    heads(right)
    from_across.wait_recv()

    def finish(k, buf, j):
        a = [att[k, h] for h in range(HEADS)]
        total = sum(jnp.sum(p, axis=-1, keepdims=True) for p in a)
        squares = sum(jnp.sum(p * p, axis=-1, keepdims=True) for p in a)
        mean = total * (1.0 / D)
        var = squares * (1.0 / D) - mean * mean
        scale = lax.rsqrt(var + EPS * float(WINDOW * WINDOW))
        gated = jnp.concatenate(
            [((p - mean) * scale * gates[k, h].astype(F32)).astype(BF16) for h, p in enumerate(a)],
            axis=1,
        )
        mixed = jnp.dot(gated, wo[...], preferred_element_type=F32) + user_rows(k)
        mixed = mixed.astype(BF16)
        last = len_s[0, mp * OWN + k] - 1
        rows = lax.broadcasted_iota(jnp.int32, (WINDOW, HEAD), 0)
        for q in range(N_MP):
            part = mixed[:, q * HEAD : (q + 1) * HEAD]
            buf[q, :, j] = part.reshape(GROUPS, TILE, HEAD)
            state = jnp.sum(jnp.where(rows == last, part.astype(F32), 0.0), axis=0, keepdims=True)
            st_send[q, pl.ds(k, 1)] = state

    def slots(c, count):
        return middle[c].at[pl.ds(0, count)]

    def wait_slots(c, count, sem):
        pltpu.make_async_copy(slots(c, count), slots(c, count), sem).wait()

    for c in range(CHUNKS):
        @pl.loop(0, UC)
        def _(j):
            head_of_user(across, c * UC + j)
            finish(c * UC + j, outgoing[c], j)

        if c == CHUNKS - 1:
            for n, other in enumerate((right, left, across)):
                pltpu.make_async_remote_copy(
                    src_ref=st_send.at[other], dst_ref=st_recv.at[mp],
                    send_sem=s_send.at[n], recv_sem=s_recv.at[n],
                    device_id=(me, other), device_id_type=MESH,
                ).start()

        @pl.loop(1, N_DP)
        def _(t):
            i = (me + 27 * t) % N_DP
            pltpu.make_async_remote_copy(
                src_ref=outgoing[c].at[(mp + shift_of(i)) % N_MP, i // 4],
                dst_ref=middle[c].at[me],
                send_sem=p1_send.at[c], recv_sem=p1_recv.at[c],
                device_id=(i, mp), device_id_type=MESH,
            ).start()

        pltpu.make_async_copy(
            outgoing[c].at[(mp + shift_of(me)) % N_MP, me // 4], middle[c].at[me], p1_loc.at[c]
        ).start()

    pltpu.make_async_copy(tab.at[pl.ds(0, N_DP - 1)], tab.at[pl.ds(0, N_DP - 1)], t_recv).wait()
    lane = lax.broadcasted_iota(jnp.int32, (1, 128), 1)

    def scan_tables(d, carry):
        pin, lens, offs = carry
        rows = tab[d]
        owners = rows[1:2]
        first = jnp.broadcast_to(owners[:, 0:1], (1, 128))
        mine = owners == me
        return (
            jnp.where(first == lane, d, pin),
            jnp.where(mine, rows[0:1], lens),
            jnp.where(mine, rows[2:3], offs),
        )

    zero_row = jnp.zeros((1, 128), jnp.int32)
    pin, lens, offs = lax.fori_loop(0, N_DP, scan_tables, (zero_row, zero_row, zero_row))
    pin_v[...] = pin
    meta[...] = jnp.zeros((8, 128), jnp.int32)
    meta[0:1] = lens
    meta[1:2] = offs
    to_scalars = pltpu.make_async_copy(pin_v, pin_s, pin_sem)
    to_scalars.start()
    to_scalars.wait()

    beta = shift_of(me)
    column = (mp + beta) % N_MP

    for c in range(CHUNKS):
        wait_slots(c, N_DP - 1, p1_recv.at[c])
        pltpu.make_async_copy(
            outgoing[c].at[(mp + shift_of(me)) % N_MP, me // 4], middle[c].at[me], p1_loc.at[c]
        ).wait()
        firsts = [
            own_s[0, mp * OWN + c * UC + j] - own_s[0, 0] for j in range(UC)
        ]

        @pl.loop(0, N_DP, unroll=4)
        def _(o):
            for j in range(UC):
                d = pin_s[0, (o - firsts[j]) & (N_DP - 1)]
                packed[c][o, j] = middle[c][d, j]

        dst = landed.at[me, pl.ds(c * UC, UC)]

        @pl.loop(1, N_DP)
        def _(t):
            o = (me + 27 * t) % N_DP
            pltpu.make_async_remote_copy(
                src_ref=packed[c].at[o], dst_ref=dst,
                send_sem=p2_send.at[c], recv_sem=p2_recv.at[c],
                device_id=(o, column), device_id_type=MESH,
            ).start()

        @pl.when(beta != 0)
        def _():
            pltpu.make_async_remote_copy(
                src_ref=packed[c].at[me], dst_ref=dst,
                send_sem=p2_send.at[c], recv_sem=p2_recv.at[c],
                device_id=(me, column), device_id_type=MESH,
            ).start()

        @pl.when(beta == 0)
        def _():
            pltpu.make_async_copy(packed[c].at[me], dst, p2_loc.at[c]).start()

    for n, other in enumerate((left, right, across)):
        pltpu.make_async_remote_copy(
            src_ref=st_send.at[other], dst_ref=st_recv.at[other],
            send_sem=s_send.at[n], recv_sem=s_recv.at[n],
            device_id=(me, other), device_id_type=MESH,
        ).wait()
    states[...] = st_recv[...]
    states[mp] = st_send[mp]

    for copy in (to_right, to_left, onward, from_left, from_right, from_across):
        copy.wait_send()
    pltpu.make_async_copy(tab.at[pl.ds(0, N_DP - 1)], tab.at[pl.ds(0, N_DP - 1)], t_send).wait()
    for c in range(CHUNKS):
        wait_slots(c, N_DP - 1, p1_send.at[c])

    for c in range(CHUNKS):
        @pl.when(beta != 0)
        def _():
            wait_slots(c, N_DP, p2_recv.at[c])
            wait_slots(c, N_DP, p2_send.at[c])

        @pl.when(beta == 0)
        def _():
            wait_slots(c, N_DP - 1, p2_recv.at[c])
            wait_slots(c, N_DP - 1, p2_send.at[c])
            pltpu.make_async_copy(
                packed[c].at[me], landed.at[me, pl.ds(c * UC, UC)], p2_loc.at[c]
            ).wait()


def unpack_kernel(landed, meta, states, out, state_out):
    mp = lax.axis_index("mp")

    @pl.loop(0, BLK_DEV)
    def _(b):
        out[pl.ds(b * 8, 8)] = jnp.zeros((8, TILE, HEAD), BF16)

    row = lax.broadcasted_iota(jnp.int32, (TILE, HEAD), 0)

    @pl.loop(0, USERS)
    def _(u):
        count = meta[0, u]
        first = meta[1, u]
        j = u % OWN
        delta = (mp - u // OWN + N_MP) % N_MP
        low = delta // 2 + 2 * (delta % 2)
        for s in range(2):
            @pl.when(count > s * BLOCK)
            def _():
                for r in range(8):
                    g = s * 8 + r
                    value = landed[4 * g + low, j].astype(F32)
                    value = jnp.where(row + g * TILE < count, value, 0.0)
                    out[(first + s) * 8 + r] = value.astype(BF16)

    for m in range(N_MP):
        for k in range(OWN):
            state_out[pl.ds(m * OWN + k, 1)] = states[m, pl.ds(k, 1)].astype(BF16)


def per_device(tokens, w_uvqk, w_out, hist_len, owner, recv_offset, block_start):
    any_spec = pl.BlockSpec(memory_space=pl.ANY)
    vmem = pl.BlockSpec(memory_space=pltpu.VMEM)
    smem = pl.BlockSpec(memory_space=pltpu.SMEM)
    dma = pltpu.SemaphoreType.DMA
    landed, meta, states = pl.pallas_call(
        main_kernel,
        out_shape=(
            jax.ShapeDtypeStruct((N_DP, OWN, TILE, HEAD), BF16),
            jax.ShapeDtypeStruct((8, 128), jnp.int32),
            jax.ShapeDtypeStruct((N_MP, 8, HEAD), F32),
        ),
        in_specs=[any_spec] * 3 + [vmem] * 3 + [smem] * 3,
        out_specs=(any_spec, vmem, vmem),
        scratch_shapes=[
            pltpu.VMEM((BLK_DEV, BLOCK, D), BF16),
            pltpu.VMEM((N_MP, D, D), BF16),
            pltpu.VMEM((D, D), BF16),
            pltpu.VMEM((OWN, WINDOW, D), BF16),
            pltpu.VMEM((OWN, HEADS, WINDOW, HEAD), F32),
            pltpu.VMEM((OWN, HEADS, WINDOW, HEAD), BF16),
            pltpu.VMEM((N_DP, 4, 128), jnp.int32),
            pltpu.VMEM((1, 128), jnp.int32),
            pltpu.SMEM((1, 128), jnp.int32),
            pltpu.VMEM((N_MP, 8, HEAD), F32),
            pltpu.VMEM((N_MP, 8, HEAD), F32),
        ]
        + [pltpu.VMEM((N_MP, GROUPS, UC, TILE, HEAD), BF16)] * CHUNKS
        + [pltpu.VMEM((N_DP, UC, TILE, HEAD), BF16)] * (2 * CHUNKS)
        + [
            dma((3,)), dma((3,)), dma((3,)), dma((3,)), dma((3,)), dma, dma, dma((3,)), dma((3,)),
            dma((CHUNKS,)), dma((CHUNKS,)), dma((CHUNKS,)),
            dma((CHUNKS,)), dma((CHUNKS,)), dma((CHUNKS,)), dma,
        ],
        compiler_params=pltpu.CompilerParams(collective_id=0, has_side_effects=True),
        name="layer_and_repack",
    )(
        tokens.reshape(BLK_DEV, BLOCK, D), w_uvqk, w_out,
        hist_len, owner, recv_offset, hist_len, owner, block_start,
    )
    packed, state = pl.pallas_call(
        unpack_kernel,
        out_shape=(
            jax.ShapeDtypeStruct((BLK_DEV * 8, TILE, HEAD), BF16),
            jax.ShapeDtypeStruct((USERS, HEAD), BF16),
        ),
        in_specs=[vmem, smem, vmem],
        out_specs=(vmem, vmem),
        name="unpack",
    )(landed, meta, states)
    return packed.reshape(BLK_DEV * BLOCK, HEAD), state


def solution(mesh):
    in_specs = (
        P("dp", None),
        P(None, "mp"),
        P(),
        P("dp", None),
        P("dp", None),
        P("dp", None),
        P("dp", None),
    )
    out_specs = (P("dp", "mp"), P("dp", "mp"))
    return jax.shard_map(
        per_device, mesh=mesh, in_specs=in_specs, out_specs=out_specs, check_vma=False
    )
```

time: 372 us -> 111 us (0.30)
  blocking collectives: 126 us -> 0 us
  Pallas kernels: 0 us -> 110 us
  waiting for transfers between devices: 62.4 us -> 0 us
  matrix products: 45 us -> 0 us
  loops' own time: 37.9 us -> 0 us
  local copies, waits for them, and re-layouts: 35.9 us -> 0 us
  other arithmetic: 33.7 us -> 0 us
  starting transfers between devices: 16 us -> 0 us
  between operations: 14.3 us -> 0.64 us
    all_gather x1 -> x0, blocking collectives: 126 us -> none  [in_one_piece(): result = lax.all_gather(both, axis, axis=dim, tiled=True)]
    pallas_call x0 -> x2, Pallas kernels: none -> 110 us  [the longest x1 106 us: per_device(): pl.pallas_call(main_kernel, out_shape=(jax.ShapeDtypeStruct((N_DP, OWN, T...]
    all_gather x1 -> x0, waiting for transfers between devices: 60.7 us -> none  [layer_rows(): every_head = lax.all_gather(gated_rows, 'mp', axis=1, tiled=True)]
    dot_general x14 -> x0, matrix products: 45 us -> none  [the longest x12 31.4 us: one_tile(): return jnp.dot(weights, value_tile, preferred_element_type=jnp.float32)]
    another operation x1 -> x0, loops' own time: 37.9 us -> none  [attend(): return lax.map(one_tile, tile_starts).reshape(row_count, head_size)]
    all_to_all x2 -> x0, starting transfers between devices: 16 us -> none  [the longest x1 11.2 us: per_device(): lax.all_to_all(outgoing, 'dp', split_axis=0, concat_axis=0, tiled=True)]
    convert_element_type x2 -> x0, other arithmetic: 13.1 us -> none  [the longest x1 9.17 us: layer_rows(): widened = rows_in.astype(jnp.float32)]
    select_n x8 -> x0, other arithmetic: 10.6 us -> none  [the longest x1 5.24 us: per_device(): packed = jnp.where(owned_live[:, None], gathered, jnp.zeros_like(gathered))]
  transfers between devices with their start and end apart: 3 -> 0, of which waited for: 2 -> 0; matrix products, arithmetic and copies ran while one was open for 4% -> 0% of each run, Pallas kernels for 0% -> 0%
where the time goes in v1:
time: 111 us; the launch traced here: 110 us
  Pallas kernels  110 us (99%)
    pallas_call x1, Pallas kernels, per_device(): pl.pallas_call(main_kernel, out_shape=(jax.ShapeDtypeStruct((N_DP, OWN, T...  106 us
    pallas_call x1, Pallas kernels, per_device(): pl.pallas_call(unpack_kernel, out_shape=(jax.ShapeDtypeStruct((BLK_DEV *...  4.09 us

profile of v1, /device:TPU:1, one launch (start us, length us, event | category | flops | bytes accessed | tf_op | source)
XLA Modules:
  0.0 110.5 jit_solution(5586576350078855927)
XLA Ops:
  0.6 105.7 %layer_and_repack.1 = (bf16[64,6,16,128]{3,2,1,0:T(8,128)(2,1)}, s32[8,128]{1,0:T(8,128)}, f32[4,8,128]{2,1,0:T(8,128)}) custom-call(bf16[48,128,512]{2,1,0:T(8,128)(2,1)} %bitcast.2, bf16[512,512]{1,0:T(8,128)(2,1)} %w_in.1, bf16[512,512]{1,0:T(8,128)(2,1)} %w_out.1, s32[1,24]{1,0:T(1,128)} %len_s.1, s32[1,24]{1,0:T(1,128)} %own_s.1, s32[1,24]{1,0:T(1,128)} %off_v.1, ...), custom_call_target="tpu_custom_call" | custom-call | tf_op jit(solution)/shard_map/layer_and_repack/pallas_call | solution.py:368
  106.4 4.1 %unpack.1 = (bf16[384,16,128]{2,1,0:T(8,128)(2,1)}, bf16[24,128]{1,0:T(8,128)(2,1)}) custom-call(bf16[64,6,16,128]{3,2,1,0:T(8,128)(2,1)} %get-tuple-element.7.landed, s32[8,128]{1,0:T(8,128)} %get-tuple-element.8.meta, f32[4,8,128]{2,1,0:T(8,128)} %get-tuple-element.9.states), custom_call_target="tpu_custom_call" | custom-call | tf_op jit(solution)/shard_map/unpack/pallas_call | solution.py:403

commit v2 on v1

v2 whole, which is shorter than its diff:
```python
import functools

import jax
import jax.numpy as jnp
from jax import lax
from jax.experimental import pallas as pl
from jax.experimental.pallas import tpu as pltpu
from jax.sharding import PartitionSpec as P

D = 512
HEADS = 4
HEAD = 128
BLOCK = 128
WINDOW = 256
USERS = 24
BLK_DEV = 48
N_DP = 64
N_MP = 4
OWN = USERS // N_MP
EARLY = 3
LATE = OWN - EARLY
TILE = 16
GROUPS = WINDOW // TILE
EPS = 1e-05
MESH = pl.DeviceIdType.MESH
BF16 = jnp.bfloat16
F32 = jnp.float32


def shift_of(i):
    return 2 * (i % 2) + (i // 2) % 2


def gated_silu(v):
    half = v * 0.5
    return half + half * jnp.tanh(half)


def main_kernel(
    tokens, w_in, w_out, len_v, own_v, off_v, len_s, own_s, start_s,
    landed, landed_early, meta, states,
    tok, wbuf, wo, normed, att, gates, x_early, mix_early, tab, build, pin_v, pin_s, st_send, st_recv,
    out_early, mid_early, pack_early, in_early, out_late, mid_late, pack_late,
    loc_sem, w_send, w_recv, f_send, f_recv, t_send, t_recv, s_send, s_recv,
    e1_send, e1_recv, e1_loc, e2_send, e2_recv, e2_loc, x_send, x_recv, x_loc,
    l1_send, l1_recv, l1_loc, l2_send, l2_recv, l2_loc, pin_sem,
):
    me = lax.axis_index("dp")
    mp = lax.axis_index("mp")
    core = me % 2
    partner = me + 1 - 2 * core
    right = (mp + 1) % N_MP
    left = (mp + 3) % N_MP
    across = (mp + 2) % N_MP

    load_tok = pltpu.make_async_copy(tokens, tok, loc_sem.at[0])
    load_w = pltpu.make_async_copy(w_in, wbuf.at[mp], loc_sem.at[1])
    load_wo = pltpu.make_async_copy(w_out, wo, loc_sem.at[2])
    load_w.start()
    load_tok.start()
    load_wo.start()

    barrier = pltpu.get_barrier_semaphore()

    @pl.loop(1, N_DP)
    def _(t):
        pl.semaphore_signal(barrier, inc=1, device_id=((me + t) % N_DP, mp), device_id_type=MESH)

    for other in (right, left, across):
        pl.semaphore_signal(barrier, inc=1, device_id=(me, other), device_id_type=MESH)

    build[...] = jnp.zeros_like(build)
    build[0:1, 0:USERS] = len_v[...]
    build[1:2, 0:USERS] = own_v[...]
    build[2:3, 0:USERS] = off_v[...]
    tab[me] = (
        build[0:1]
        + pltpu.roll(build[1:2], USERS, 1)
        + pltpu.roll(build[2:3], 2 * USERS, 1)
    )
    st_send[...] = jnp.zeros_like(st_send)

    load_tok.wait()

    def user_blocks(k):
        start = start_s[0, mp * OWN + k]
        return tok[start], tok[jnp.minimum(start + 1, BLK_DEV - 1)]

    def user_rows(k):
        return jnp.concatenate(user_blocks(k), axis=0).astype(F32)

    for k in range(EARLY):
        for s, block in enumerate(user_blocks(k)):
            for q in range(N_MP):
                part = block[:, q * HEAD : (q + 1) * HEAD]
                out_early[q, s * 8 : s * 8 + 8, k] = part.reshape(8, TILE, HEAD)

    def normalize(k, x):
        mean = jnp.mean(x, axis=-1, keepdims=True)
        var = jnp.mean(x * x, axis=-1, keepdims=True) - mean * mean
        normed[k] = ((x - mean) * lax.rsqrt(var + EPS)).astype(BF16)

    @pl.loop(0, OWN)
    def _(k):
        normalize(k, user_rows(k))

    load_w.wait()
    load_wo.wait()
    pl.semaphore_wait(barrier, N_DP - 1 + N_MP - 1)

    half = pl.ds(pl.multiple_of(core * 256, 256), 256)

    def send_w(shard, target, k):
        return pltpu.make_async_remote_copy(
            src_ref=wbuf.at[shard, half], dst_ref=wbuf.at[shard, half],
            send_sem=w_send.at[k], recv_sem=w_recv.at[k],
            device_id=(me, target), device_id_type=MESH,
        )

    def forward_w(shard, k):
        return pltpu.make_async_remote_copy(
            src_ref=wbuf.at[shard, half], dst_ref=wbuf.at[shard, half],
            send_sem=f_send.at[k], recv_sem=f_recv.at[k],
            device_id=(partner, mp), device_id_type=MESH,
        )

    to_right = send_w(mp, right, 0)
    to_left = send_w(mp, left, 1)
    to_right.start()
    to_left.start()

    @pl.loop(1, N_DP)
    def _(t):
        pltpu.make_async_remote_copy(
            src_ref=tab.at[me], dst_ref=tab.at[me], send_sem=t_send, recv_sem=t_recv,
            device_id=((me + t) % N_DP, mp), device_id_type=MESH,
        ).start()

    @pl.loop(1, N_DP)
    def _(t):
        i = (me + 27 * t) % N_DP
        pltpu.make_async_remote_copy(
            src_ref=out_early.at[i % 4, i // 4], dst_ref=mid_early.at[me],
            send_sem=e1_send, recv_sem=e1_recv,
            device_id=(i, mp), device_id_type=MESH,
        ).start()

    own_early = pltpu.make_async_copy(out_early.at[me % 4, me // 4], mid_early.at[me], e1_loc)
    own_early.start()

    row_id = lax.broadcasted_iota(jnp.int32, (BLOCK, BLOCK), 0)
    col_id = lax.broadcasted_iota(jnp.int32, (BLOCK, BLOCK), 1)
    causal = col_id <= row_id
    scaling = float(HEAD) ** -0.5
    nt = (((1,), (1,)), ((), ()))

    def head_of_user(shard, k):
        projected = gated_silu(
            jnp.dot(normed[k], wbuf[shard], preferred_element_type=F32)
        ).astype(BF16)
        gates[k, shard] = projected[:, 0:HEAD]
        v = projected[:, HEAD : 2 * HEAD]
        q = projected[:, 2 * HEAD : 3 * HEAD]
        key = projected[:, 3 * HEAD :]
        diag = jnp.concatenate(
            [
                lax.dot_general(q[:BLOCK], key[:BLOCK], nt, preferred_element_type=F32),
                lax.dot_general(q[BLOCK:], key[BLOCK:], nt, preferred_element_type=F32),
            ],
            axis=0,
        )
        back = lax.dot_general(q[BLOCK:], key[:BLOCK], nt, preferred_element_type=F32)
        both = jnp.concatenate([causal, causal], axis=0)
        w_diag = jnp.where(both, gated_silu(diag * scaling), 0.0).astype(BF16)
        w_back = gated_silu(back * scaling).astype(BF16)
        att[k, shard, 0:BLOCK] = jnp.dot(w_diag[:BLOCK], v[:BLOCK], preferred_element_type=F32)
        att[k, shard, BLOCK:] = jnp.dot(
            jnp.concatenate([w_back, w_diag[BLOCK:]], axis=1), v, preferred_element_type=F32
        )

    def heads(shard, low, high):
        @pl.loop(low, high)
        def _(k):
            head_of_user(shard, k)

    def finish(k, x):
        a = [att[k, h] for h in range(HEADS)]
        total = sum(jnp.sum(p, axis=-1, keepdims=True) for p in a)
        squares = sum(jnp.sum(p * p, axis=-1, keepdims=True) for p in a)
        mean = total * (1.0 / D)
        var = squares * (1.0 / D) - mean * mean
        scale = lax.rsqrt(var + EPS * float(WINDOW * WINDOW))
        gated = jnp.concatenate(
            [((p - mean) * scale * gates[k, h].astype(F32)).astype(BF16) for h, p in enumerate(a)],
            axis=1,
        )
        mixed = jnp.dot(gated, wo[...], preferred_element_type=F32) + x
        return mixed.astype(BF16)

    def keep_state(k, mixed):
        last = len_s[0, mp * OWN + k] - 1
        rows = lax.broadcasted_iota(jnp.int32, (WINDOW, HEAD), 0)
        for q in range(N_MP):
            part = mixed[:, q * HEAD : (q + 1) * HEAD].astype(F32)
            state = jnp.sum(jnp.where(rows == last, part, 0.0), axis=0, keepdims=True)
            st_send[q, pl.ds(k, 1)] = state

    heads(mp, EARLY, OWN)

    to_right.wait_recv()
    from_left = forward_w(left, 0)
    from_left.start()
    to_left.wait_recv()
    from_right = forward_w(right, 1)
    from_right.start()
    onward_shard = jnp.where(core == 0, left, right)
    onward_target = jnp.where(core == 0, right, left)
    onward = send_w(onward_shard, onward_target, 2)
    onward.start()
    from_left.wait_recv()
    heads(left, EARLY, OWN)
    from_right.wait_recv()
    heads(right, EARLY, OWN)
    onward.wait_recv()
    from_across = forward_w(across, 2)
    from_across.start()
    from_across.wait_recv()

    @pl.loop(0, LATE)
    def _(j):
        k = EARLY + j
        head_of_user(across, k)
        mixed = finish(k, user_rows(k))
        for q in range(N_MP):
            part = mixed[:, q * HEAD : (q + 1) * HEAD]
            out_late[q, :, j] = part.reshape(GROUPS, TILE, HEAD)
        keep_state(k, mixed)

    @pl.loop(1, N_DP)
    def _(t):
        i = (me + 27 * t) % N_DP
        pltpu.make_async_remote_copy(
            src_ref=out_late.at[(mp + shift_of(i)) % N_MP, i // 4], dst_ref=mid_late.at[me],
            send_sem=l1_send, recv_sem=l1_recv,
            device_id=(i, mp), device_id_type=MESH,
        ).start()

    own_late = pltpu.make_async_copy(
        out_late.at[(mp + shift_of(me)) % N_MP, me // 4], mid_late.at[me], l1_loc
    )
    own_late.start()

    def wait_slots(ref, count, sem):
        some = ref.at[pl.ds(0, count)]
        pltpu.make_async_copy(some, some, sem).wait()

    wait_slots(tab, N_DP - 1, t_recv)
    lane = lax.broadcasted_iota(jnp.int32, (1, 128), 1)

    def scan_tables(d, carry):
        pin, lens, offs = carry
        rows = tab[d]
        owners = pltpu.roll(rows, 128 - USERS, 1)
        first = jnp.broadcast_to(owners[:, 0:1], (1, 128))
        mine = owners == me
        return (
            jnp.where(first == lane, d, pin),
            jnp.where(mine, rows, lens),
            jnp.where(mine, pltpu.roll(rows, 128 - 2 * USERS, 1), offs),
        )

    zero_row = jnp.zeros((1, 128), jnp.int32)
    pin, lens, offs = lax.fori_loop(
        0, N_DP, scan_tables, (zero_row, zero_row, zero_row), unroll=4
    )
    pin_v[...] = pin
    meta[...] = jnp.zeros((8, 128), jnp.int32)
    meta[0:1] = lens
    meta[1:2] = offs
    to_scalars = pltpu.make_async_copy(pin_v, pin_s, pin_sem)
    to_scalars.start()
    to_scalars.wait()

    def regroup(packed, middle, low, count):
        firsts = [own_s[0, mp * OWN + low + j] - own_s[0, 0] for j in range(count)]

        @pl.loop(0, N_DP, unroll=4)
        def _(o):
            for j in range(count):
                packed[o, j] = middle[pin_s[0, (o - firsts[j]) & (N_DP - 1)], j]

    wait_slots(mid_early, N_DP - 1, e1_recv)
    own_early.wait()
    regroup(pack_early, mid_early, 0, EARLY)

    @pl.loop(1, N_DP)
    def _(t):
        o = (me + 27 * t) % N_DP
        pltpu.make_async_remote_copy(
            src_ref=pack_early.at[o], dst_ref=in_early.at[me],
            send_sem=e2_send, recv_sem=e2_recv,
            device_id=(o, mp), device_id_type=MESH,
        ).start()

    kept_early = pltpu.make_async_copy(pack_early.at[me], in_early.at[me], e2_loc)
    kept_early.start()

    for shard in (mp, left, right):
        heads(shard, 0, EARLY)

    @pl.loop(0, EARLY)
    def _(k):
        head_of_user(across, k)
        keep_state(k, finish(k, user_rows(k)))

    state_copies = []
    for n, (other, source) in enumerate(((right, left), (left, right), (across, across))):
        copy = pltpu.make_async_remote_copy(
            src_ref=st_send.at[other], dst_ref=st_recv.at[mp],
            send_sem=s_send.at[n], recv_sem=s_recv.at[n],
            device_id=(me, other), device_id_type=MESH,
        )
        copy.start()
        state_copies.append(copy)

    beta = shift_of(me)
    column = (mp + beta) % N_MP
    wait_slots(mid_late, N_DP - 1, l1_recv)
    own_late.wait()
    regroup(pack_late, mid_late, EARLY, LATE)

    @pl.loop(1, N_DP)
    def _(t):
        o = (me + 27 * t) % N_DP
        pltpu.make_async_remote_copy(
            src_ref=pack_late.at[o], dst_ref=landed.at[me],
            send_sem=l2_send, recv_sem=l2_recv,
            device_id=(o, column), device_id_type=MESH,
        ).start()

    @pl.when(beta != 0)
    def _():
        pltpu.make_async_remote_copy(
            src_ref=pack_late.at[me], dst_ref=landed.at[me],
            send_sem=l2_send, recv_sem=l2_recv,
            device_id=(me, column), device_id_type=MESH,
        ).start()

    @pl.when(beta == 0)
    def _():
        pltpu.make_async_copy(pack_late.at[me], landed.at[me], l2_loc).start()

    wait_slots(in_early, N_DP - 1, e2_recv)
    kept_early.wait()

    @pl.loop(0, GROUPS)
    def _(g):
        rows = pl.ds(pl.multiple_of(g * TILE, TILE), TILE)
        for q in range(N_MP):
            for k in range(EARLY):
                x_early[k, rows, q * HEAD : (q + 1) * HEAD] = in_early[4 * g + q, k]

    for k in range(EARLY):
        normalize(k, x_early[k].astype(F32))

    for shard in (mp, left, right):
        heads(shard, 0, EARLY)

    for k in range(EARLY):
        head_of_user(across, k)
        mixed = finish(k, x_early[k].astype(F32))
        for q in range(N_MP):
            mix_early[q, k] = mixed[:, q * HEAD : (q + 1) * HEAD]
        for n, other in enumerate((right, left, across)):
            pltpu.make_async_remote_copy(
                src_ref=mix_early.at[other, k], dst_ref=landed_early.at[mp, k],
                send_sem=x_send.at[n], recv_sem=x_recv.at[n],
                device_id=(me, other), device_id_type=MESH,
            ).start()

    kept = pltpu.make_async_copy(mix_early.at[mp], landed_early.at[mp], x_loc)
    kept.start()

    for copy in state_copies:
        copy.wait()
    for m in range(N_MP):
        @pl.when(m != mp)
        def _():
            states[m] = st_recv[m]

        @pl.when(m == mp)
        def _():
            states[m] = st_send[m]

    for copy in (to_right, to_left, onward, from_left, from_right, from_across):
        copy.wait_send()
    wait_slots(tab, N_DP - 1, t_send)
    wait_slots(mid_early, N_DP - 1, e1_send)
    wait_slots(mid_early, N_DP - 1, e2_send)
    wait_slots(mid_late, N_DP - 1, l1_send)
    for n, (other, source) in enumerate(((right, left), (left, right), (across, across))):
        pltpu.make_async_remote_copy(
            src_ref=mix_early.at[other], dst_ref=landed_early.at[source],
            send_sem=x_send.at[n], recv_sem=x_recv.at[n],
            device_id=(me, other), device_id_type=MESH,
        ).wait()
    kept.wait()

    @pl.when(beta != 0)
    def _():
        wait_slots(mid_late, N_DP, l2_recv)
        wait_slots(mid_late, N_DP, l2_send)

    @pl.when(beta == 0)
    def _():
        wait_slots(mid_late, N_DP - 1, l2_recv)
        wait_slots(mid_late, N_DP - 1, l2_send)
        pltpu.make_async_copy(pack_late.at[me], landed.at[me], l2_loc).wait()


def unpack_kernel(landed, landed_early, meta, states, out, state_out):
    mp = lax.axis_index("mp")

    @pl.loop(0, BLK_DEV)
    def _(b):
        out[pl.ds(b * 8, 8)] = jnp.zeros((8, TILE, HEAD), BF16)

    row = lax.broadcasted_iota(jnp.int32, (TILE, HEAD), 0)

    def place(u, g, value):
        count = meta[0, u]
        value = jnp.where(row + g * TILE < count, value.astype(F32), 0.0)
        out[meta[1, u] * 8 + g] = value.astype(BF16)

    for m in range(N_MP):
        delta = (mp - m + N_MP) % N_MP
        low = delta // 2 + 2 * (delta % 2)

        @pl.loop(0, OWN)
        def _(k):
            u = m * OWN + k
            for s in range(2):
                @pl.when((meta[0, u] > s * BLOCK) & (k < EARLY))
                def _():
                    for r in range(8):
                        g = s * 8 + r
                        place(u, g, landed_early[m, k, g])

                @pl.when((meta[0, u] > s * BLOCK) & (k >= EARLY))
                def _():
                    for r in range(8):
                        g = s * 8 + r
                        place(u, g, landed[4 * g + low, k - EARLY])

    for m in range(N_MP):
        for k in range(OWN):
            state_out[pl.ds(m * OWN + k, 1)] = states[m, pl.ds(k, 1)].astype(BF16)


def per_device(tokens, w_uvqk, w_out, hist_len, owner, recv_offset, block_start):
    any_spec = pl.BlockSpec(memory_space=pl.ANY)
    vmem = pl.BlockSpec(memory_space=pltpu.VMEM)
    smem = pl.BlockSpec(memory_space=pltpu.SMEM)
    dma = pltpu.SemaphoreType.DMA
    landed, landed_early, meta, states = pl.pallas_call(
        main_kernel,
        out_shape=(
            jax.ShapeDtypeStruct((N_DP, LATE, TILE, HEAD), BF16),
            jax.ShapeDtypeStruct((N_MP, EARLY, WINDOW, HEAD), BF16),
            jax.ShapeDtypeStruct((8, 128), jnp.int32),
            jax.ShapeDtypeStruct((N_MP, 8, HEAD), F32),
        ),
        in_specs=[any_spec] * 3 + [vmem] * 3 + [smem] * 3,
        out_specs=(any_spec, any_spec, vmem, vmem),
        scratch_shapes=[
            pltpu.VMEM((BLK_DEV, BLOCK, D), BF16),
            pltpu.VMEM((N_MP, D, D), BF16),
            pltpu.VMEM((D, D), BF16),
            pltpu.VMEM((OWN, WINDOW, D), BF16),
            pltpu.VMEM((OWN, HEADS, WINDOW, HEAD), F32),
            pltpu.VMEM((OWN, HEADS, WINDOW, HEAD), BF16),
            pltpu.VMEM((EARLY, WINDOW, D), BF16),
            pltpu.VMEM((N_MP, EARLY, WINDOW, HEAD), BF16),
            pltpu.VMEM((N_DP, 1, 128), jnp.int32),
            pltpu.VMEM((8, 128), jnp.int32),
            pltpu.VMEM((1, 128), jnp.int32),
            pltpu.SMEM((1, 128), jnp.int32),
            pltpu.VMEM((N_MP, 8, HEAD), F32),
            pltpu.VMEM((N_MP, 8, HEAD), F32),
            pltpu.VMEM((N_MP, GROUPS, EARLY, TILE, HEAD), BF16),
            pltpu.VMEM((N_DP, EARLY, TILE, HEAD), BF16),
            pltpu.VMEM((N_DP, EARLY, TILE, HEAD), BF16),
            pltpu.VMEM((N_DP, EARLY, TILE, HEAD), BF16),
            pltpu.VMEM((N_MP, GROUPS, LATE, TILE, HEAD), BF16),
            pltpu.VMEM((N_DP, LATE, TILE, HEAD), BF16),
            pltpu.VMEM((N_DP, LATE, TILE, HEAD), BF16),
            dma((3,)), dma((3,)), dma((3,)), dma((3,)), dma((3,)), dma, dma, dma((3,)), dma((3,)),
            dma, dma, dma, dma, dma, dma, dma((3,)), dma((3,)), dma,
            dma, dma, dma, dma, dma, dma, dma,
        ],
        compiler_params=pltpu.CompilerParams(collective_id=0, has_side_effects=True),
        name="layer_and_repack",
    )(
        tokens.reshape(BLK_DEV, BLOCK, D), w_uvqk, w_out,
        hist_len, owner, recv_offset, hist_len, owner, block_start,
    )
    packed, state = pl.pallas_call(
        unpack_kernel,
        out_shape=(
            jax.ShapeDtypeStruct((BLK_DEV * 8, TILE, HEAD), BF16),
            jax.ShapeDtypeStruct((USERS, HEAD), BF16),
        ),
        in_specs=[vmem, vmem, smem, vmem],
        out_specs=(vmem, vmem),
        name="unpack",
    )(landed, landed_early.reshape(N_MP, EARLY, GROUPS, TILE, HEAD), meta, states)
    return packed.reshape(BLK_DEV * BLOCK, HEAD), state


def solution(mesh):
    in_specs = (
        P("dp", None),
        P(None, "mp"),
        P(),
        P("dp", None),
        P("dp", None),
        P("dp", None),
        P("dp", None),
    )
    out_specs = (P("dp", "mp"), P("dp", "mp"))
    return jax.shard_map(
        per_device, mesh=mesh, in_specs=in_specs, out_specs=out_specs, check_vma=False
    )
```

time: 111 us -> 96.3 us (0.87)
  Pallas kernels: 110 us -> 95.6 us
    pallas_call x1, Pallas kernels: 106 us -> 91.2 us  [per_device(): pl.pallas_call(main_kernel, out_shape=(jax.ShapeDtypeStruct((N_DP, LATE,...]
where the time goes in v2:
time: 96.3 us; the launch traced here: 96.2 us
  Pallas kernels  95.6 us (99%)
    pallas_call x1, Pallas kernels, per_device(): pl.pallas_call(main_kernel, out_shape=(jax.ShapeDtypeStruct((N_DP, LATE,...  91.2 us
    pallas_call x1, Pallas kernels, per_device(): pl.pallas_call(unpack_kernel, out_shape=(jax.ShapeDtypeStruct((BLK_DEV *...  4.37 us

profile of v2, /device:TPU:1, one launch (start us, length us, event | category | flops | bytes accessed | tf_op | source)
XLA Modules:
  0.0 96.2 jit_solution(5933131313850571620)
XLA Ops:
  0.6 91.2 %layer_and_repack.1 = (bf16[64,3,16,128]{3,2,1,0:T(8,128)(2,1)}, bf16[4,3,256,128]{3,2,1,0:T(8,128)(2,1)}, s32[8,128]{1,0:T(8,128)}, f32[4,8,128]{2,1,0:T(8,128)}) custom-call(bf16[48,128,512]{2,1,0:T(8,128)(2,1)} %bitcast.3, bf16[512,512]{1,0:T(8,128)(2,1)} %w_in.1, bf16[512,512]{1,0:T(8,128)(2,1)} %w_out.1, s32[1,24]{1,0:T(1,128)} %len_s.1, ...), custom_call_target="tpu_custom_call" | custom-call | tf_op jit(solution)/shard_map/layer_and_repack/pallas_call | solution.py:465
  91.8 4.4 %unpack.1 = (bf16[384,16,128]{2,1,0:T(8,128)(2,1)}, bf16[24,128]{1,0:T(8,128)(2,1)}) custom-call(bf16[64,3,16,128]{3,2,1,0:T(8,128)(2,1)} %get-tuple-element.8.landed, bf16[4,3,16,16,128]{4,3,2,1,0:T(8,128)(2,1)} %bitcast.4, s32[8,128]{1,0:T(8,128)} %get-tuple-element.10.meta, f32[4,8,128]{2,1,0:T(8,128)} %get-tuple-element.11.states), custom_call_target="tpu_custom_call" | custom-call | tf_op jit(solution)/shard_map/unpack/pallas_call | solution.py:507

commit v3 on v2

--- a/solution.py
+++ b/solution.py
@@ -17,7 +17,10 @@
 N_DP = 64
 N_MP = 4
 OWN = USERS // N_MP
-EARLY = 3
+PARTS = (2, 1)
+EARLY = sum(PARTS)
+CHUNKS = len(PARTS)
+STARTS = tuple(sum(PARTS[:c]) for c in range(CHUNKS))
 LATE = OWN - EARLY
 TILE = 16
 GROUPS = WINDOW // TILE
@@ -37,14 +40,17 @@
 
 
 def main_kernel(
-    tokens, w_in, w_out, len_v, own_v, off_v, len_s, own_s, start_s,
+    tokens, w_in, w_out, len_in, own_in, off_in, start_in,
     landed, landed_early, meta, states,
     tok, wbuf, wo, normed, att, gates, x_early, mix_early, tab, build, pin_v, pin_s, st_send, st_recv,
-    out_early, mid_early, pack_early, in_early, out_late, mid_late, pack_late,
-    loc_sem, w_send, w_recv, f_send, f_recv, t_send, t_recv, s_send, s_recv,
+    len_v, own_v, off_v, len_s, own_s, start_s, out_late, mid_late, pack_late, *rest,
+):
+    out_early, mid_early, pack_early, in_early = (
+        rest[n * CHUNKS : (n + 1) * CHUNKS] for n in range(4)
+    )
+    (loc_sem, in_sem, w_send, w_recv, f_send, f_recv, t_send, t_recv, s_send, s_recv,
     e1_send, e1_recv, e1_loc, e2_send, e2_recv, e2_loc, x_send, x_recv, x_loc,
-    l1_send, l1_recv, l1_loc, l2_send, l2_recv, l2_loc, pin_sem,
-):
+    l1_send, l1_recv, l1_loc, l2_send, l2_recv, l2_loc, pin_sem) = rest[4 * CHUNKS :]
     me = lax.axis_index("dp")
     mp = lax.axis_index("mp")
     core = me % 2
@@ -54,20 +60,40 @@
     across = (mp + 2) % N_MP
 
     load_tok = pltpu.make_async_copy(tokens, tok, loc_sem.at[0])
+    load_tok.start()
+    small = [
+        pltpu.make_async_copy(src, dst, in_sem.at[n])
+        for n, (src, dst) in enumerate(
+            (
+                (start_in, start_s), (len_in, len_v), (own_in, own_v), (off_in, off_v),
+                (len_in, len_s), (own_in, own_s),
+            )
+        )
+    ]
     load_w = pltpu.make_async_copy(w_in, wbuf.at[mp], loc_sem.at[1])
     load_wo = pltpu.make_async_copy(w_out, wo, loc_sem.at[2])
+    for copy in small:
+        copy.start()
     load_w.start()
-    load_tok.start()
     load_wo.start()
 
     barrier = pltpu.get_barrier_semaphore()
 
-    @pl.loop(1, N_DP)
+    def greet(peer):
+        pl.semaphore_signal(barrier, inc=1, device_id=(peer % N_DP, mp), device_id_type=MESH)
+
+    greet(me + N_DP // 2)
+
+    @pl.loop(1, N_DP // 2)
     def _(t):
-        pl.semaphore_signal(barrier, inc=1, device_id=((me + t) % N_DP, mp), device_id_type=MESH)
+        greet(me + N_DP // 2 + t)
+        greet(me + N_DP // 2 - t)
 
     for other in (right, left, across):
         pl.semaphore_signal(barrier, inc=1, device_id=(me, other), device_id_type=MESH)
+
+    for copy in small:
+        copy.wait()
 
     build[...] = jnp.zeros_like(build)
     build[0:1, 0:USERS] = len_v[...]
@@ -93,19 +119,10 @@
         for s, block in enumerate(user_blocks(k)):
             for q in range(N_MP):
                 part = block[:, q * HEAD : (q + 1) * HEAD]
-                out_early[q, s * 8 : s * 8 + 8, k] = part.reshape(8, TILE, HEAD)
-
-    def normalize(k, x):
-        mean = jnp.mean(x, axis=-1, keepdims=True)
-        var = jnp.mean(x * x, axis=-1, keepdims=True) - mean * mean
-        normed[k] = ((x - mean) * lax.rsqrt(var + EPS)).astype(BF16)
-
-    @pl.loop(0, OWN)
-    def _(k):
-        normalize(k, user_rows(k))
+                c = sum(k >= low for low in STARTS) - 1
+                out_early[c][q, s * 8 : s * 8 + 8, k - STARTS[c]] = part.reshape(8, TILE, HEAD)
 
     load_w.wait()
-    load_wo.wait()
     pl.semaphore_wait(barrier, N_DP - 1 + N_MP - 1)
 
     half = pl.ds(pl.multiple_of(core * 256, 256), 256)
@@ -129,24 +146,42 @@
     to_right.start()
     to_left.start()
 
-    @pl.loop(1, N_DP)
-    def _(t):
-        pltpu.make_async_remote_copy(
-            src_ref=tab.at[me], dst_ref=tab.at[me], send_sem=t_send, recv_sem=t_recv,
-            device_id=((me + t) % N_DP, mp), device_id_type=MESH,
-        ).start()
-
-    @pl.loop(1, N_DP)
-    def _(t):
-        i = (me + 27 * t) % N_DP
-        pltpu.make_async_remote_copy(
-            src_ref=out_early.at[i % 4, i // 4], dst_ref=mid_early.at[me],
-            send_sem=e1_send, recv_sem=e1_recv,
-            device_id=(i, mp), device_id_type=MESH,
-        ).start()
-
-    own_early = pltpu.make_async_copy(out_early.at[me % 4, me // 4], mid_early.at[me], e1_loc)
-    own_early.start()
+    def send_tables():
+        @pl.loop(1, N_DP)
+        def _(t):
+            pltpu.make_async_remote_copy(
+                src_ref=tab.at[me], dst_ref=tab.at[me], send_sem=t_send, recv_sem=t_recv,
+                device_id=((me + t) % N_DP, mp), device_id_type=MESH,
+            ).start()
+
+    own_early = []
+    for c in range(CHUNKS):
+        @pl.loop(1, N_DP)
+        def _(t):
+            i = (me + 27 * t) % N_DP
+            pltpu.make_async_remote_copy(
+                src_ref=out_early[c].at[i % 4, i // 4], dst_ref=mid_early[c].at[me],
+                send_sem=e1_send.at[c], recv_sem=e1_recv.at[c],
+                device_id=(i, mp), device_id_type=MESH,
+            ).start()
+
+        copy = pltpu.make_async_copy(
+            out_early[c].at[me % 4, me // 4], mid_early[c].at[me], e1_loc.at[c]
+        )
+        copy.start()
+        own_early.append(copy)
+        if c == 0:
+            send_tables()
+
+    load_wo.wait()
+    def normalize(k, x):
+        mean = jnp.mean(x, axis=-1, keepdims=True)
+        var = jnp.mean(x * x, axis=-1, keepdims=True) - mean * mean
+        normed[k] = ((x - mean) * lax.rsqrt(var + EPS)).astype(BF16)
+
+    @pl.loop(EARLY, OWN)
+    def _(k):
+        normalize(k, user_rows(k))
 
     row_id = lax.broadcasted_iota(jnp.int32, (BLOCK, BLOCK), 0)
     col_id = lax.broadcasted_iota(jnp.int32, (BLOCK, BLOCK), 1)
@@ -183,6 +218,8 @@
         def _(k):
             head_of_user(shard, k)
 
+    heads(mp, EARLY, OWN)
+
     def finish(k, x):
         a = [att[k, h] for h in range(HEADS)]
         total = sum(jnp.sum(p, axis=-1, keepdims=True) for p in a)
@@ -204,8 +241,6 @@
             part = mixed[:, q * HEAD : (q + 1) * HEAD].astype(F32)
             state = jnp.sum(jnp.where(rows == last, part, 0.0), axis=0, keepdims=True)
             st_send[q, pl.ds(k, 1)] = state
-
-    heads(mp, EARLY, OWN)
 
     to_right.wait_recv()
     from_left = forward_w(left, 0)
@@ -236,43 +271,46 @@
             out_late[q, :, j] = part.reshape(GROUPS, TILE, HEAD)
         keep_state(k, mixed)
 
+    def send_late(i, hop):
+        column = (mp + hop) % N_MP
+        pltpu.make_async_remote_copy(
+            src_ref=out_late.at[column, i // 4], dst_ref=mid_late.at[me],
+            send_sem=l1_send, recv_sem=l1_recv,
+            device_id=(i, column), device_id_type=MESH,
+        ).start()
+
     @pl.loop(1, N_DP)
     def _(t):
         i = (me + 27 * t) % N_DP
-        pltpu.make_async_remote_copy(
-            src_ref=out_late.at[(mp + shift_of(i)) % N_MP, i // 4], dst_ref=mid_late.at[me],
-            send_sem=l1_send, recv_sem=l1_recv,
-            device_id=(i, mp), device_id_type=MESH,
-        ).start()
-
-    own_late = pltpu.make_async_copy(
-        out_late.at[(mp + shift_of(me)) % N_MP, me // 4], mid_late.at[me], l1_loc
-    )
-    own_late.start()
+        send_late(i, shift_of(i))
+
+    hop = shift_of(me)
+
+    @pl.when(hop != 0)
+    def _():
+        send_late(me, hop)
+
+    @pl.when(hop == 0)
+    def _():
+        pltpu.make_async_copy(out_late.at[mp, me // 4], mid_late.at[me], l1_loc).start()
 
     def wait_slots(ref, count, sem):
         some = ref.at[pl.ds(0, count)]
         pltpu.make_async_copy(some, some, sem).wait()
 
     wait_slots(tab, N_DP - 1, t_recv)
-    lane = lax.broadcasted_iota(jnp.int32, (1, 128), 1)
-
-    def scan_tables(d, carry):
-        pin, lens, offs = carry
-        rows = tab[d]
-        owners = pltpu.roll(rows, 128 - USERS, 1)
-        first = jnp.broadcast_to(owners[:, 0:1], (1, 128))
-        mine = owners == me
-        return (
-            jnp.where(first == lane, d, pin),
-            jnp.where(mine, rows, lens),
-            jnp.where(mine, pltpu.roll(rows, 128 - 2 * USERS, 1), offs),
-        )
-
-    zero_row = jnp.zeros((1, 128), jnp.int32)
-    pin, lens, offs = lax.fori_loop(
-        0, N_DP, scan_tables, (zero_row, zero_row, zero_row), unroll=4
-    )
+    rows = tab[...].reshape(N_DP, 128)
+    owners = pltpu.roll(rows, 128 - USERS, 1)
+    offsets = pltpu.roll(rows, 128 - 2 * USERS, 1)
+    lane = lax.broadcasted_iota(jnp.int32, (N_DP, 128), 1)
+    source = lax.broadcasted_iota(jnp.int32, (N_DP, 128), 0)
+
+    def pick(mask, values):
+        return jnp.max(jnp.where(mask, values, 0), axis=0, keepdims=True)
+
+    pin = pick(owners[:, 0:1] == lane, source)
+    lens = pick(owners == me, rows)
+    offs = pick(owners == me, offsets)
     pin_v[...] = pin
     meta[...] = jnp.zeros((8, 128), jnp.int32)
     meta[0:1] = lens
@@ -282,28 +320,35 @@
     to_scalars.wait()
 
     def regroup(packed, middle, low, count):
-        firsts = [own_s[0, mp * OWN + low + j] - own_s[0, 0] for j in range(count)]
+        firsts = [own_s[0, low + j] - own_s[0, 0] for j in range(count)]
 
         @pl.loop(0, N_DP, unroll=4)
         def _(o):
             for j in range(count):
                 packed[o, j] = middle[pin_s[0, (o - firsts[j]) & (N_DP - 1)], j]
 
-    wait_slots(mid_early, N_DP - 1, e1_recv)
-    own_early.wait()
-    regroup(pack_early, mid_early, 0, EARLY)
-
-    @pl.loop(1, N_DP)
-    def _(t):
-        o = (me + 27 * t) % N_DP
-        pltpu.make_async_remote_copy(
-            src_ref=pack_early.at[o], dst_ref=in_early.at[me],
-            send_sem=e2_send, recv_sem=e2_recv,
-            device_id=(o, mp), device_id_type=MESH,
-        ).start()
-
-    kept_early = pltpu.make_async_copy(pack_early.at[me], in_early.at[me], e2_loc)
-    kept_early.start()
+    kept_early = []
+    for c in range(CHUNKS):
+        wait_slots(mid_early[c], N_DP - 1, e1_recv.at[c])
+        own_early[c].wait()
+        regroup(pack_early[c], mid_early[c], mp * OWN + STARTS[c], PARTS[c])
+
+        @pl.loop(1, N_DP)
+        def _(t):
+            o = (me + 27 * t) % N_DP
+            pltpu.make_async_remote_copy(
+                src_ref=pack_early[c].at[o], dst_ref=in_early[c].at[me],
+                send_sem=e2_send.at[c], recv_sem=e2_recv.at[c],
+                device_id=(o, mp), device_id_type=MESH,
+            ).start()
+
+        copy = pltpu.make_async_copy(pack_early[c].at[me], in_early[c].at[me], e2_loc.at[c])
+        copy.start()
+        kept_early.append(copy)
+
+    @pl.loop(0, EARLY)
+    def _(k):
+        normalize(k, user_rows(k))
 
     for shard in (mp, left, right):
         heads(shard, 0, EARLY)
@@ -323,11 +368,16 @@
         copy.start()
         state_copies.append(copy)
 
-    beta = shift_of(me)
-    column = (mp + beta) % N_MP
-    wait_slots(mid_late, N_DP - 1, l1_recv)
-    own_late.wait()
-    regroup(pack_late, mid_late, EARLY, LATE)
+    @pl.when(hop != 0)
+    def _():
+        wait_slots(mid_late, N_DP, l1_recv)
+
+    @pl.when(hop == 0)
+    def _():
+        wait_slots(mid_late, N_DP - 1, l1_recv)
+        pltpu.make_async_copy(out_late.at[mp, me // 4], mid_late.at[me], l1_loc).wait()
+
+    regroup(pack_late, mid_late, (mp - hop + N_MP) % N_MP * OWN + EARLY, LATE)
 
     @pl.loop(1, N_DP)
     def _(t):
@@ -335,48 +385,42 @@
         pltpu.make_async_remote_copy(
             src_ref=pack_late.at[o], dst_ref=landed.at[me],
             send_sem=l2_send, recv_sem=l2_recv,
-            device_id=(o, column), device_id_type=MESH,
+            device_id=(o, mp), device_id_type=MESH,
         ).start()
 
-    @pl.when(beta != 0)
-    def _():
-        pltpu.make_async_remote_copy(
-            src_ref=pack_late.at[me], dst_ref=landed.at[me],
-            send_sem=l2_send, recv_sem=l2_recv,
-            device_id=(me, column), device_id_type=MESH,
-        ).start()
-
-    @pl.when(beta == 0)
-    def _():
-        pltpu.make_async_copy(pack_late.at[me], landed.at[me], l2_loc).start()
-
-    wait_slots(in_early, N_DP - 1, e2_recv)
-    kept_early.wait()
-
-    @pl.loop(0, GROUPS)
-    def _(g):
-        rows = pl.ds(pl.multiple_of(g * TILE, TILE), TILE)
-        for q in range(N_MP):
-            for k in range(EARLY):
-                x_early[k, rows, q * HEAD : (q + 1) * HEAD] = in_early[4 * g + q, k]
-
-    for k in range(EARLY):
-        normalize(k, x_early[k].astype(F32))
-
-    for shard in (mp, left, right):
-        heads(shard, 0, EARLY)
-
-    for k in range(EARLY):
-        head_of_user(across, k)
-        mixed = finish(k, x_early[k].astype(F32))
-        for q in range(N_MP):
-            mix_early[q, k] = mixed[:, q * HEAD : (q + 1) * HEAD]
-        for n, other in enumerate((right, left, across)):
-            pltpu.make_async_remote_copy(
-                src_ref=mix_early.at[other, k], dst_ref=landed_early.at[mp, k],
-                send_sem=x_send.at[n], recv_sem=x_recv.at[n],
-                device_id=(me, other), device_id_type=MESH,
-            ).start()
+    kept_late = pltpu.make_async_copy(pack_late.at[me], landed.at[me], l2_loc)
+    kept_late.start()
+
+    for c in range(CHUNKS):
+        wait_slots(in_early[c], N_DP - 1, e2_recv.at[c])
+        kept_early[c].wait()
+        mine = range(STARTS[c], STARTS[c] + PARTS[c])
+
+        @pl.loop(0, GROUPS)
+        def _(g):
+            rows = pl.ds(pl.multiple_of(g * TILE, TILE), TILE)
+            for q in range(N_MP):
+                for k in mine:
+                    x_early[k, rows, q * HEAD : (q + 1) * HEAD] = in_early[c][4 * g + q, k - STARTS[c]]
+
+        for k in mine:
+            normalize(k, x_early[k].astype(F32))
+
+        for shard in (mp, left, right):
+            heads(shard, mine[0], mine[0] + PARTS[c])
+
+        @pl.loop(mine[0], mine[0] + PARTS[c])
+        def _(k):
+            head_of_user(across, k)
+            mixed = finish(k, x_early[k].astype(F32))
+            for q in range(N_MP):
+                mix_early[q, k] = mixed[:, q * HEAD : (q + 1) * HEAD]
+            for n, other in enumerate((right, left, across)):
+                pltpu.make_async_remote_copy(
+                    src_ref=mix_early.at[other, k], dst_ref=landed_early.at[mp, k],
+                    send_sem=x_send.at[n], recv_sem=x_recv.at[n],
+                    device_id=(me, other), device_id_type=MESH,
+                ).start()
 
     kept = pltpu.make_async_copy(mix_early.at[mp], landed_early.at[mp], x_loc)
     kept.start()
@@ -395,9 +439,19 @@
     for copy in (to_right, to_left, onward, from_left, from_right, from_across):
         copy.wait_send()
     wait_slots(tab, N_DP - 1, t_send)
-    wait_slots(mid_early, N_DP - 1, e1_send)
-    wait_slots(mid_early, N_DP - 1, e2_send)
-    wait_slots(mid_late, N_DP - 1, l1_send)
+    for c in range(CHUNKS):
+        wait_slots(mid_early[c], N_DP - 1, e1_send.at[c])
+        wait_slots(mid_early[c], N_DP - 1, e2_send.at[c])
+
+    @pl.when(hop != 0)
+    def _():
+        wait_slots(mid_late, N_DP, l1_send)
+
+    @pl.when(hop == 0)
+    def _():
+        wait_slots(mid_late, N_DP - 1, l1_send)
+
+    wait_slots(mid_late, N_DP - 1, l2_send)
     for n, (other, source) in enumerate(((right, left), (left, right), (across, across))):
         pltpu.make_async_remote_copy(
             src_ref=mix_early.at[other], dst_ref=landed_early.at[source],
@@ -406,16 +460,8 @@
         ).wait()
     kept.wait()
 
-    @pl.when(beta != 0)
-    def _():
-        wait_slots(mid_late, N_DP, l2_recv)
-        wait_slots(mid_late, N_DP, l2_send)
-
-    @pl.when(beta == 0)
-    def _():
-        wait_slots(mid_late, N_DP - 1, l2_recv)
-        wait_slots(mid_late, N_DP - 1, l2_send)
-        pltpu.make_async_copy(pack_late.at[me], landed.at[me], l2_loc).wait()
+    wait_slots(mid_late, N_DP - 1, l2_recv)
+    kept_late.wait()
 
 
 def unpack_kernel(landed, landed_early, meta, states, out, state_out):
@@ -470,8 +516,8 @@
             jax.ShapeDtypeStruct((8, 128), jnp.int32),
             jax.ShapeDtypeStruct((N_MP, 8, HEAD), F32),
         ),
-        in_specs=[any_spec] * 3 + [vmem] * 3 + [smem] * 3,
-        out_specs=(any_spec, any_spec, vmem, vmem),
+        in_specs=[any_spec] * 7,
+        out_specs=(vmem, vmem, vmem, vmem),
         scratch_shapes=[
             pltpu.VMEM((BLK_DEV, BLOCK, D), BF16),
             pltpu.VMEM((N_MP, D, D), BF16),
@@ -487,22 +533,24 @@
             pltpu.SMEM((1, 128), jnp.int32),
             pltpu.VMEM((N_MP, 8, HEAD), F32),
             pltpu.VMEM((N_MP, 8, HEAD), F32),
-            pltpu.VMEM((N_MP, GROUPS, EARLY, TILE, HEAD), BF16),
-            pltpu.VMEM((N_DP, EARLY, TILE, HEAD), BF16),
-            pltpu.VMEM((N_DP, EARLY, TILE, HEAD), BF16),
-            pltpu.VMEM((N_DP, EARLY, TILE, HEAD), BF16),
+            *[pltpu.VMEM((1, USERS), jnp.int32)] * 3,
+            *[pltpu.SMEM((1, USERS), jnp.int32)] * 3,
             pltpu.VMEM((N_MP, GROUPS, LATE, TILE, HEAD), BF16),
             pltpu.VMEM((N_DP, LATE, TILE, HEAD), BF16),
             pltpu.VMEM((N_DP, LATE, TILE, HEAD), BF16),
-            dma((3,)), dma((3,)), dma((3,)), dma((3,)), dma((3,)), dma, dma, dma((3,)), dma((3,)),
-            dma, dma, dma, dma, dma, dma, dma((3,)), dma((3,)), dma,
+        ]
+        + [pltpu.VMEM((N_MP, GROUPS, part, TILE, HEAD), BF16) for part in PARTS]
+        + [pltpu.VMEM((N_DP, part, TILE, HEAD), BF16) for part in PARTS * 3]
+        + [
+            dma((3,)), dma((6,)), dma((3,)), dma((3,)), dma((3,)), dma((3,)), dma, dma, dma((3,)), dma((3,)),
+            *[dma((CHUNKS,))] * 6, dma((3,)), dma((3,)), dma,
             dma, dma, dma, dma, dma, dma, dma,
         ],
         compiler_params=pltpu.CompilerParams(collective_id=0, has_side_effects=True),
         name="layer_and_repack",
     )(
         tokens.reshape(BLK_DEV, BLOCK, D), w_uvqk, w_out,
-        hist_len, owner, recv_offset, hist_len, owner, block_start,
+        hist_len, owner, recv_offset, block_start,
     )
     packed, state = pl.pallas_call(
         unpack_kernel,

time: 96.3 us -> 90.8 us (0.943)
  Pallas kernels: 95.6 us -> 90.1 us
    pallas_call x1, Pallas kernels: 91.2 us -> 85.7 us  [per_device(): pl.pallas_call(main_kernel, out_shape=(jax.ShapeDtypeStruct((N_DP, LATE,...]
where the time goes in v3:
time: 90.8 us; the launch traced here: 90.7 us
  Pallas kernels  90.1 us (99%)
    pallas_call x1, Pallas kernels, per_device(): pl.pallas_call(main_kernel, out_shape=(jax.ShapeDtypeStruct((N_DP, LATE,...  85.7 us
    pallas_call x1, Pallas kernels, per_device(): pl.pallas_call(unpack_kernel, out_shape=(jax.ShapeDtypeStruct((BLK_DEV *...  4.36 us

profile of v3, /device:TPU:1, one launch (start us, length us, event | category | flops | bytes accessed | tf_op | source)
XLA Modules:
  0.0 90.7 jit_solution(17731791980764323466)
XLA Ops:
  0.6 85.7 %layer_and_repack.1 = (bf16[64,3,16,128]{3,2,1,0:T(8,128)(2,1)}, bf16[4,3,256,128]{3,2,1,0:T(8,128)(2,1)}, s32[8,128]{1,0:T(8,128)}, f32[4,8,128]{2,1,0:T(8,128)}) custom-call(bf16[48,128,512]{2,1,0:T(8,128)(2,1)} %bitcast.3, bf16[512,512]{1,0:T(8,128)(2,1)} %w_in.1, bf16[512,512]{1,0:T(8,128)(2,1)} %w_out.1, s32[1,24]{1,0:T(1,128)} %len_in.1, ...), custom_call_target="tpu_custom_call" | custom-call | tf_op jit(solution)/shard_map/layer_and_repack/pallas_call | solution.py:511
  86.4 4.4 %unpack.1 = (bf16[384,16,128]{2,1,0:T(8,128)(2,1)}, bf16[24,128]{1,0:T(8,128)(2,1)}) custom-call(bf16[64,3,16,128]{3,2,1,0:T(8,128)(2,1)} %get-tuple-element.8.landed, bf16[4,3,16,16,128]{4,3,2,1,0:T(8,128)(2,1)} %bitcast.4, s32[8,128]{1,0:T(8,128)} %get-tuple-element.10.meta, f32[4,8,128]{2,1,0:T(8,128)} %get-tuple-element.11.states), custom_call_target="tpu_custom_call" | custom-call | tf_op jit(solution)/shard_map/unpack/pallas_call | solution.py:555

commit v4 on v3

--- a/solution.py
+++ b/solution.py
@@ -232,13 +232,17 @@
             axis=1,
         )
         mixed = jnp.dot(gated, wo[...], preferred_element_type=F32) + x
-        return mixed.astype(BF16)
+        return mixed
+
+    def live_rows(mixed, count):
+        rows = lax.broadcasted_iota(jnp.int32, (WINDOW, D), 0)
+        return jnp.where(rows < count, mixed, 0.0).astype(BF16)
 
     def keep_state(k, mixed):
         last = len_s[0, mp * OWN + k] - 1
         rows = lax.broadcasted_iota(jnp.int32, (WINDOW, HEAD), 0)
         for q in range(N_MP):
-            part = mixed[:, q * HEAD : (q + 1) * HEAD].astype(F32)
+            part = mixed[:, q * HEAD : (q + 1) * HEAD].astype(BF16).astype(F32)
             state = jnp.sum(jnp.where(rows == last, part, 0.0), axis=0, keepdims=True)
             st_send[q, pl.ds(k, 1)] = state
 
@@ -266,10 +270,11 @@
         k = EARLY + j
         head_of_user(across, k)
         mixed = finish(k, user_rows(k))
+        keep_state(k, mixed)
+        mixed = live_rows(mixed, len_s[0, mp * OWN + k])
         for q in range(N_MP):
             part = mixed[:, q * HEAD : (q + 1) * HEAD]
             out_late[q, :, j] = part.reshape(GROUPS, TILE, HEAD)
-        keep_state(k, mixed)
 
     def send_late(i, hop):
         column = (mp + hop) % N_MP
@@ -311,7 +316,9 @@
     pin = pick(owners[:, 0:1] == lane, source)
     lens = pick(owners == me, rows)
     offs = pick(owners == me, offsets)
-    pin_v[...] = pin
+    pin_v[...] = jnp.zeros((8, 128), jnp.int32)
+    pin_v[0:1] = pin
+    pin_v[1:2] = lens
     meta[...] = jnp.zeros((8, 128), jnp.int32)
     meta[0:1] = lens
     meta[1:2] = offs
@@ -412,7 +419,7 @@
         @pl.loop(mine[0], mine[0] + PARTS[c])
         def _(k):
             head_of_user(across, k)
-            mixed = finish(k, x_early[k].astype(F32))
+            mixed = live_rows(finish(k, x_early[k].astype(F32)), pin_s[1, mp * OWN + k])
             for q in range(N_MP):
                 mix_early[q, k] = mixed[:, q * HEAD : (q + 1) * HEAD]
             for n, other in enumerate((right, left, across)):
@@ -464,43 +471,50 @@
     kept_late.wait()
 
 
-def unpack_kernel(landed, landed_early, meta, states, out, state_out):
+def unpack_kernel(landed, landed_early, meta, states, out, state_out, zeros, block_of, sem):
     mp = lax.axis_index("mp")
+    zeros[...] = jnp.zeros_like(zeros)
+
+    @pl.loop(0, BLK_DEV, unroll=8)
+    def _(b):
+        block_of[0, b] = -1
+
+    for m in range(N_MP):
+        for k in range(OWN):
+            u = m * OWN + k
+            code = (m * 8 + k) * 2
+            first = meta[1, u]
+            block_of[0, first] = code
+
+            @pl.when(meta[0, u] > BLOCK)
+            def _():
+                block_of[0, first + 1] = code + 1
 
     @pl.loop(0, BLK_DEV)
     def _(b):
-        out[pl.ds(b * 8, 8)] = jnp.zeros((8, TILE, HEAD), BF16)
-
-    row = lax.broadcasted_iota(jnp.int32, (TILE, HEAD), 0)
-
-    def place(u, g, value):
-        count = meta[0, u]
-        value = jnp.where(row + g * TILE < count, value.astype(F32), 0.0)
-        out[meta[1, u] * 8 + g] = value.astype(BF16)
-
-    for m in range(N_MP):
-        delta = (mp - m + N_MP) % N_MP
-        low = delta // 2 + 2 * (delta % 2)
-
-        @pl.loop(0, OWN)
-        def _(k):
-            u = m * OWN + k
-            for s in range(2):
-                @pl.when((meta[0, u] > s * BLOCK) & (k < EARLY))
-                def _():
-                    for r in range(8):
-                        g = s * 8 + r
-                        place(u, g, landed_early[m, k, g])
-
-                @pl.when((meta[0, u] > s * BLOCK) & (k >= EARLY))
-                def _():
-                    for r in range(8):
-                        g = s * 8 + r
-                        place(u, g, landed[4 * g + low, k - EARLY])
+        code = block_of[0, b]
+        m = (code >> 4) & 3
+        k = (code >> 1) & 7
+        groups = pl.ds((code & 1) * 8, 8)
+
+        @pl.when(code < 0)
+        def _():
+            pltpu.make_async_copy(zeros, out.at[b], sem).start()
+
+        @pl.when((code >= 0) & (k < EARLY))
+        def _():
+            pltpu.make_async_copy(landed_early.at[m, k, groups], out.at[b], sem).start()
+
+        @pl.when((code >= 0) & (k >= EARLY))
+        def _():
+            delta = (mp - m) & 3
+            low = (delta >> 1) + 2 * (delta & 1)
+            pltpu.make_async_copy(landed.at[groups, low, k - EARLY], out.at[b], sem).start()
 
     for m in range(N_MP):
         for k in range(OWN):
             state_out[pl.ds(m * OWN + k, 1)] = states[m, pl.ds(k, 1)].astype(BF16)
+    pltpu.make_async_copy(out, out, sem).wait()
 
 
 def per_device(tokens, w_uvqk, w_out, hist_len, owner, recv_offset, block_start):
@@ -517,7 +531,7 @@
             jax.ShapeDtypeStruct((N_MP, 8, HEAD), F32),
         ),
         in_specs=[any_spec] * 7,
-        out_specs=(vmem, vmem, vmem, vmem),
+        out_specs=(any_spec, any_spec, vmem, vmem),
         scratch_shapes=[
             pltpu.VMEM((BLK_DEV, BLOCK, D), BF16),
             pltpu.VMEM((N_MP, D, D), BF16),
@@ -529,8 +543,8 @@
             pltpu.VMEM((N_MP, EARLY, WINDOW, HEAD), BF16),
             pltpu.VMEM((N_DP, 1, 128), jnp.int32),
             pltpu.VMEM((8, 128), jnp.int32),
-            pltpu.VMEM((1, 128), jnp.int32),
-            pltpu.SMEM((1, 128), jnp.int32),
+            pltpu.VMEM((8, 128), jnp.int32),
+            pltpu.SMEM((8, 128), jnp.int32),
             pltpu.VMEM((N_MP, 8, HEAD), F32),
             pltpu.VMEM((N_MP, 8, HEAD), F32),
             *[pltpu.VMEM((1, USERS), jnp.int32)] * 3,
@@ -546,22 +560,35 @@
             *[dma((CHUNKS,))] * 6, dma((3,)), dma((3,)), dma,
             dma, dma, dma, dma, dma, dma, dma,
         ],
-        compiler_params=pltpu.CompilerParams(collective_id=0, has_side_effects=True),
+        compiler_params=pltpu.CompilerParams(
+            collective_id=0, has_side_effects=True, vmem_limit_bytes=40 * 2**20
+        ),
         name="layer_and_repack",
     )(
-        tokens.reshape(BLK_DEV, BLOCK, D), w_uvqk, w_out,
-        hist_len, owner, recv_offset, block_start,
+        *(
+            pltpu.with_memory_space_constraint(a, pltpu.HBM)
+            for a in (
+                tokens.reshape(BLK_DEV, BLOCK, D), w_uvqk, w_out,
+                hist_len, owner, recv_offset, block_start,
+            )
+        )
     )
     packed, state = pl.pallas_call(
         unpack_kernel,
         out_shape=(
-            jax.ShapeDtypeStruct((BLK_DEV * 8, TILE, HEAD), BF16),
+            jax.ShapeDtypeStruct((BLK_DEV, 8, TILE, HEAD), BF16),
             jax.ShapeDtypeStruct((USERS, HEAD), BF16),
         ),
-        in_specs=[vmem, vmem, smem, vmem],
-        out_specs=(vmem, vmem),
+        in_specs=[any_spec, any_spec, smem, vmem],
+        out_specs=(any_spec, vmem),
+        scratch_shapes=[pltpu.VMEM((8, TILE, HEAD), BF16), pltpu.SMEM((1, 128), jnp.int32), dma],
+        compiler_params=pltpu.CompilerParams(vmem_limit_bytes=16 * 2**20),
         name="unpack",
-    )(landed, landed_early.reshape(N_MP, EARLY, GROUPS, TILE, HEAD), meta, states)
+    )(
+        landed.reshape(GROUPS, N_MP, LATE, TILE, HEAD),
+        landed_early.reshape(N_MP, EARLY, GROUPS, TILE, HEAD),
+        meta, states,
+    )
     return packed.reshape(BLK_DEV * BLOCK, HEAD), state
 
 

time: 90.8 us -> 88.1 us (0.970)
  Pallas kernels: 90.1 us -> 87.4 us
    pallas_call x1, Pallas kernels: 4.36 us -> 2.72 us  [per_device(): pl.pallas_call(unpack_kernel, out_shape=(jax.ShapeDtypeStruct((BLK_DEV, 8...]
    pallas_call x1, Pallas kernels: 85.7 us -> 84.7 us  [per_device(): pl.pallas_call(main_kernel, out_shape=(jax.ShapeDtypeStruct((N_DP, LATE,...]
where the time goes in v4:
time: 88.1 us; the launch traced here: 88 us
  Pallas kernels  87.4 us (99%)
    pallas_call x1, Pallas kernels, per_device(): pl.pallas_call(main_kernel, out_shape=(jax.ShapeDtypeStruct((N_DP, LATE,...  84.7 us
    pallas_call x1, Pallas kernels, per_device(): pl.pallas_call(unpack_kernel, out_shape=(jax.ShapeDtypeStruct((BLK_DEV, 8...  2.72 us

profile of v4, /device:TPU:1, one launch (start us, length us, event | category | flops | bytes accessed | tf_op | source)
XLA Modules:
  0.0 88.0 jit_solution(4520796148584216885)
XLA Ops:
  0.6 84.7 %layer_and_repack.1 = (bf16[64,3,16,128]{3,2,1,0:T(8,128)(2,1)S(1)}, bf16[4,3,256,128]{3,2,1,0:T(8,128)(2,1)S(1)}, s32[8,128]{1,0:T(8,128)S(1)}, f32[4,8,128]{2,1,0:T(8,128)S(1)}) custom-call(bf16[48,128,512]{2,1,0:T(8,128)(2,1)} %bitcast.6, bf16[512,512]{1,0:T(8,128)(2,1)} %w_in.1, bf16[512,512]{1,0:T(8,128)(2,1)} %w_out.1, s32[1,24]{1,0:T(1,128)} %len_in.1, ...), custom_call_target="tpu_custom_call" | custom-call | tf_op jit(solution)/shard_map/layer_and_repack/pallas_call | solution.py:525
  85.3 2.7 %unpack.1 = (bf16[48,8,16,128]{3,2,1,0:T(8,128)(2,1)}, bf16[24,128]{1,0:T(8,128)(2,1)}) custom-call(bf16[16,4,3,16,128]{4,3,2,1,0:T(8,128)(2,1)S(1)} %bitcast.4, bf16[4,3,16,16,128]{4,3,2,1,0:T(8,128)(2,1)S(1)} %bitcast.5, s32[8,128]{1,0:T(8,128)S(1)} %get-tuple-element.10.meta, f32[4,8,128]{2,1,0:T(8,128)S(1)} %get-tuple-element.11.states), custom_call_target="tpu_custom_call" | custom-call | tf_op jit(solution)/shard_map/unpack/pallas_call | solution.py:576

commit v5 on v4

--- a/solution.py
+++ b/solution.py
@@ -17,7 +17,7 @@
 N_DP = 64
 N_MP = 4
 OWN = USERS // N_MP
-PARTS = (2, 1)
+PARTS = (1, 2)
 EARLY = sum(PARTS)
 CHUNKS = len(PARTS)
 STARTS = tuple(sum(PARTS[:c]) for c in range(CHUNKS))
@@ -260,45 +260,6 @@
     heads(left, EARLY, OWN)
     from_right.wait_recv()
     heads(right, EARLY, OWN)
-    onward.wait_recv()
-    from_across = forward_w(across, 2)
-    from_across.start()
-    from_across.wait_recv()
-
-    @pl.loop(0, LATE)
-    def _(j):
-        k = EARLY + j
-        head_of_user(across, k)
-        mixed = finish(k, user_rows(k))
-        keep_state(k, mixed)
-        mixed = live_rows(mixed, len_s[0, mp * OWN + k])
-        for q in range(N_MP):
-            part = mixed[:, q * HEAD : (q + 1) * HEAD]
-            out_late[q, :, j] = part.reshape(GROUPS, TILE, HEAD)
-
-    def send_late(i, hop):
-        column = (mp + hop) % N_MP
-        pltpu.make_async_remote_copy(
-            src_ref=out_late.at[column, i // 4], dst_ref=mid_late.at[me],
-            send_sem=l1_send, recv_sem=l1_recv,
-            device_id=(i, column), device_id_type=MESH,
-        ).start()
-
-    @pl.loop(1, N_DP)
-    def _(t):
-        i = (me + 27 * t) % N_DP
-        send_late(i, shift_of(i))
-
-    hop = shift_of(me)
-
-    @pl.when(hop != 0)
-    def _():
-        send_late(me, hop)
-
-    @pl.when(hop == 0)
-    def _():
-        pltpu.make_async_copy(out_late.at[mp, me // 4], mid_late.at[me], l1_loc).start()
-
     def wait_slots(ref, count, sem):
         some = ref.at[pl.ds(0, count)]
         pltpu.make_async_copy(some, some, sem).wait()
@@ -335,7 +296,8 @@
                 packed[o, j] = middle[pin_s[0, (o - firsts[j]) & (N_DP - 1)], j]
 
     kept_early = []
-    for c in range(CHUNKS):
+
+    def second_of_early(c):
         wait_slots(mid_early[c], N_DP - 1, e1_recv.at[c])
         own_early[c].wait()
         regroup(pack_early[c], mid_early[c], mp * OWN + STARTS[c], PARTS[c])
@@ -352,6 +314,49 @@
         copy = pltpu.make_async_copy(pack_early[c].at[me], in_early[c].at[me], e2_loc.at[c])
         copy.start()
         kept_early.append(copy)
+
+    onward.wait_recv()
+    from_across = forward_w(across, 2)
+    from_across.start()
+    second_of_early(0)
+    from_across.wait_recv()
+
+    @pl.loop(0, LATE)
+    def _(j):
+        k = EARLY + j
+        head_of_user(across, k)
+        mixed = finish(k, user_rows(k))
+        keep_state(k, mixed)
+        mixed = live_rows(mixed, len_s[0, mp * OWN + k])
+        for q in range(N_MP):
+            part = mixed[:, q * HEAD : (q + 1) * HEAD]
+            out_late[q, :, j] = part.reshape(GROUPS, TILE, HEAD)
+
+    def send_late(i, hop):
+        column = (mp + hop) % N_MP
+        pltpu.make_async_remote_copy(
+            src_ref=out_late.at[column, i // 4], dst_ref=mid_late.at[me],
+            send_sem=l1_send, recv_sem=l1_recv,
+            device_id=(i, column), device_id_type=MESH,
+        ).start()
+
+    @pl.loop(1, N_DP)
+    def _(t):
+        i = (me + 27 * t) % N_DP
+        send_late(i, shift_of(i))
+
+    hop = shift_of(me)
+
+    @pl.when(hop != 0)
+    def _():
+        send_late(me, hop)
+
+    @pl.when(hop == 0)
+    def _():
+        pltpu.make_async_copy(out_late.at[mp, me // 4], mid_late.at[me], l1_loc).start()
+
+    for c in range(1, CHUNKS):
+        second_of_early(c)
 
     @pl.loop(0, EARLY)
     def _(k):

time: 88.1 us -> 86.2 us (0.978)
  Pallas kernels: 87.4 us -> 85.4 us
    pallas_call x1, Pallas kernels: 84.7 us -> 82.7 us  [per_device(): pl.pallas_call(main_kernel, out_shape=(jax.ShapeDtypeStruct((N_DP, LATE,...]
where the time goes in v5:
time: 86.2 us; the launch traced here: 86.1 us
  Pallas kernels  85.4 us (99%)
    pallas_call x1, Pallas kernels, per_device(): pl.pallas_call(main_kernel, out_shape=(jax.ShapeDtypeStruct((N_DP, LATE,...  82.7 us
    pallas_call x1, Pallas kernels, per_device(): pl.pallas_call(unpack_kernel, out_shape=(jax.ShapeDtypeStruct((BLK_DEV, 8...  2.72 us

profile of v5, /device:TPU:1, one launch (start us, length us, event | category | flops | bytes accessed | tf_op | source)
XLA Modules:
  0.0 86.1 jit_solution(7983122187158035088)
XLA Ops:
  0.6 82.7 %layer_and_repack.1 = (bf16[64,3,16,128]{3,2,1,0:T(8,128)(2,1)S(1)}, bf16[4,3,256,128]{3,2,1,0:T(8,128)(2,1)S(1)}, s32[8,128]{1,0:T(8,128)S(1)}, f32[4,8,128]{2,1,0:T(8,128)S(1)}) custom-call(bf16[48,128,512]{2,1,0:T(8,128)(2,1)} %bitcast.6, bf16[512,512]{1,0:T(8,128)(2,1)} %w_in.1, bf16[512,512]{1,0:T(8,128)(2,1)} %w_out.1, s32[1,24]{1,0:T(1,128)} %len_in.1, ...), custom_call_target="tpu_custom_call" | custom-call | tf_op jit(solution)/shard_map/layer_and_repack/pallas_call | solution.py:530
  83.4 2.7 %unpack.1 = (bf16[48,8,16,128]{3,2,1,0:T(8,128)(2,1)}, bf16[24,128]{1,0:T(8,128)(2,1)}) custom-call(bf16[16,4,3,16,128]{4,3,2,1,0:T(8,128)(2,1)S(1)} %bitcast.4, bf16[4,3,16,16,128]{4,3,2,1,0:T(8,128)(2,1)S(1)} %bitcast.5, s32[8,128]{1,0:T(8,128)S(1)} %get-tuple-element.10.meta, f32[4,8,128]{2,1,0:T(8,128)S(1)} %get-tuple-element.11.states), custom_call_target="tpu_custom_call" | custom-call | tf_op jit(solution)/shard_map/unpack/pallas_call | solution.py:581

commit v6 on v5

--- a/solution.py
+++ b/solution.py
@@ -48,7 +48,7 @@
     out_early, mid_early, pack_early, in_early = (
         rest[n * CHUNKS : (n + 1) * CHUNKS] for n in range(4)
     )
-    (loc_sem, in_sem, w_send, w_recv, f_send, f_recv, t_send, t_recv, s_send, s_recv,
+    (loc_sem, tok_sem, in_sem, w_send, w_recv, f_send, f_recv, t_send, t_recv, s_send, s_recv,
     e1_send, e1_recv, e1_loc, e2_send, e2_recv, e2_loc, x_send, x_recv, x_loc,
     l1_send, l1_recv, l1_loc, l2_send, l2_recv, l2_loc, pin_sem) = rest[4 * CHUNKS :]
     me = lax.axis_index("dp")
@@ -59,8 +59,13 @@
     left = (mp + 3) % N_MP
     across = (mp + 2) % N_MP
 
-    load_tok = pltpu.make_async_copy(tokens, tok, loc_sem.at[0])
-    load_tok.start()
+    quarter = BLK_DEV // 4
+    load_tok = [
+        pltpu.make_async_copy(
+            tokens.at[pl.ds(n * quarter, quarter)], tok.at[pl.ds(n * quarter, quarter)], tok_sem.at[n]
+        )
+        for n in range(4)
+    ]
     small = [
         pltpu.make_async_copy(src, dst, in_sem.at[n])
         for n, (src, dst) in enumerate(
@@ -73,6 +78,8 @@
     load_w = pltpu.make_async_copy(w_in, wbuf.at[mp], loc_sem.at[1])
     load_wo = pltpu.make_async_copy(w_out, wo, loc_sem.at[2])
     for copy in small:
+        copy.start()
+    for copy in load_tok:
         copy.start()
     load_w.start()
     load_wo.start()
@@ -106,7 +113,8 @@
     )
     st_send[...] = jnp.zeros_like(st_send)
 
-    load_tok.wait()
+    for copy in load_tok:
+        copy.wait()
 
     def user_blocks(k):
         start = start_s[0, mp * OWN + k]
@@ -561,7 +569,7 @@
         + [pltpu.VMEM((N_MP, GROUPS, part, TILE, HEAD), BF16) for part in PARTS]
         + [pltpu.VMEM((N_DP, part, TILE, HEAD), BF16) for part in PARTS * 3]
         + [
-            dma((3,)), dma((6,)), dma((3,)), dma((3,)), dma((3,)), dma((3,)), dma, dma, dma((3,)), dma((3,)),
+            dma((3,)), dma((4,)), dma((6,)), dma((3,)), dma((3,)), dma((3,)), dma((3,)), dma, dma, dma((3,)), dma((3,)),
             *[dma((CHUNKS,))] * 6, dma((3,)), dma((3,)), dma,
             dma, dma, dma, dma, dma, dma, dma,
         ],

time: 86.2 us -> 86.2 us (level)
  no operation moved by 1% of the time
where the time goes in v6:
time: 86.2 us; the launch traced here: 86.1 us
  Pallas kernels  85.5 us (99%)
    pallas_call x1, Pallas kernels, per_device(): pl.pallas_call(main_kernel, out_shape=(jax.ShapeDtypeStruct((N_DP, LATE,...  82.8 us
    pallas_call x1, Pallas kernels, per_device(): pl.pallas_call(unpack_kernel, out_shape=(jax.ShapeDtypeStruct((BLK_DEV, 8...  2.72 us

profile of v6, /device:TPU:1, one launch (start us, length us, event | category | flops | bytes accessed | tf_op | source)
XLA Modules:
  0.0 86.1 jit_solution(5908741884490855964)
XLA Ops:
  0.6 82.8 %layer_and_repack.1 = (bf16[64,3,16,128]{3,2,1,0:T(8,128)(2,1)S(1)}, bf16[4,3,256,128]{3,2,1,0:T(8,128)(2,1)S(1)}, s32[8,128]{1,0:T(8,128)S(1)}, f32[4,8,128]{2,1,0:T(8,128)S(1)}) custom-call(bf16[48,128,512]{2,1,0:T(8,128)(2,1)} %bitcast.6, bf16[512,512]{1,0:T(8,128)(2,1)} %w_in.1, bf16[512,512]{1,0:T(8,128)(2,1)} %w_out.1, s32[1,24]{1,0:T(1,128)} %len_in.1, ...), custom_call_target="tpu_custom_call" | custom-call | tf_op jit(solution)/shard_map/layer_and_repack/pallas_call | solution.py:538
  83.4 2.7 %unpack.1 = (bf16[48,8,16,128]{3,2,1,0:T(8,128)(2,1)}, bf16[24,128]{1,0:T(8,128)(2,1)}) custom-call(bf16[16,4,3,16,128]{4,3,2,1,0:T(8,128)(2,1)S(1)} %bitcast.4, bf16[4,3,16,16,128]{4,3,2,1,0:T(8,128)(2,1)S(1)} %bitcast.5, s32[8,128]{1,0:T(8,128)S(1)} %get-tuple-element.10.meta, f32[4,8,128]{2,1,0:T(8,128)S(1)} %get-tuple-element.11.states), custom_call_target="tpu_custom_call" | custom-call | tf_op jit(solution)/shard_map/unpack/pallas_call | solution.py:589
